TPU v7x, 32 devices: a whole 2x2x4 slice. The times are simulated.
32 devices in a mesh: rows: 8 (over z, y), rank: 4 (over x, core).
Axes of the slice: x: 2, y: 2, z: 4, core: 2. Of those that a mesh axis runs over, the one named last changes fastest.
Arguments:
- left_factor: bfloat16 [128, 16384], P(None, 'rows'), may hold values from -8 to 8
- right_factor: bfloat16 [128, 16384], P(None, 'rows'), may hold values from -8 to 8
- left_plan: float32 [256, 16384], P('rank', 'rows'), may hold values from 0.0068 to 147, as said below
- right_plan: float32 [256, 16384], P('rank', 'rows'), may hold values from 0.0068 to 147, as said below
- log_inner: float32 [256], P('rank'), may hold values from -1 to 1
- left_mass: float32 [16384], P('rows'), may hold values from 32 to 1024, as said below
- right_mass: float32 [16384], P('rows'), may hold values from 32 to 1024, as said below
Outputs:
- new_left: float32 [256, 16384], P('rank', 'rows')
- new_right: float32 [256, 16384], P('rank', 'rows')
- new_log_inner: float32 [256], P('rank')
Inputs may be any that keep to these rules, and one draw needn't show every extreme that they name: `left_plan`: positive entries. `right_plan`: positive entries. `left_mass`: positive point masses. `right_mass`: positive point masses.
All inputs are finite; a program needn't handle non-finite values. Where the computation divides by a largest or mean magnitude, that divisor is 1e-20 or more.
Results may differ from a plain program's by a relative error of at most 0.00045.
Values sent between devices are 32-bit elements; how exact they have to be, the bound alone decides.
No kernel may reach another device: no remote copies, remote signals or barrier semaphores. Data moves between devices by JAX's collectives and lax.ppermute only.
A program may use at most 64 MiB of HBM per device.

v0:
```python
import jax
import jax.numpy as jnp
from jax import lax
from jax.sharding import PartitionSpec as P

RANK = 256
ITERS = 3


def contract_points(factor, plan):
    return lax.dot_general(
        factor, plan, (((1,), (1,)), ((), ())), preferred_element_type=jnp.float32
    )


def expand_points(projected, factor):
    return lax.dot_general(
        projected, factor, (((0,), (0,)), ((), ())), preferred_element_type=jnp.float32
    )


def balance(inner_mass, col_scale_left, col_total_left, col_scale_right, col_total_right):
    mixed = (
        jnp.log(inner_mass)
        + jnp.log(col_scale_left * col_total_left)
        + jnp.log(col_scale_right * col_total_right)
    )
    inner_mass = jnp.exp(mixed / 3.0)
    return (inner_mass, inner_mass / col_total_left, inner_mass / col_total_right)


def per_device(left_factor, right_factor, left_plan, right_plan, log_inner, left_mass, right_mass):
    precise = lax.Precision.HIGHEST
    columns = left_plan.shape[0]
    left_round = left_plan.astype(jnp.bfloat16)
    right_round = right_plan.astype(jnp.bfloat16)
    proj_right, proj_left, total_left, total_right = lax.psum(
        (
            contract_points(right_factor, right_round),
            contract_points(left_factor, left_round),
            jnp.sum(left_mass),
            jnp.sum(right_mass),
        ),
        "rows",
    )
    inner_mass = total_left / RANK * jnp.exp(log_inner)
    scaled_right = (proj_right / inner_mass[None, :]).astype(jnp.bfloat16)
    scaled_left = (proj_left / inner_mass[None, :]).astype(jnp.bfloat16)
    grad_left = expand_points(scaled_right, left_factor)
    grad_right = expand_points(scaled_left, right_factor)
    pairing = lax.psum(jnp.sum(left_round.astype(jnp.float32) * grad_left, axis=1), "rows")
    grad_inner = -pairing / inner_mass
    local_top = jnp.maximum(
        jnp.maximum(jnp.max(jnp.abs(grad_left)), jnp.max(jnp.abs(grad_right))),
        jnp.max(jnp.abs(grad_inner)),
    )
    largest = lax.pmax(local_top, ("rows", "rank"))
    step_size = 5.0 / jnp.maximum(largest, 0.25)
    tilted_left = left_plan * jnp.exp(-step_size * grad_left)
    tilted_right = right_plan * jnp.exp(-step_size * grad_right)
    inner_mass = inner_mass * jnp.exp(-step_size * grad_inner)
    right_norm = right_mass * (total_left / total_right)
    row_scale_left = left_mass
    row_scale_right = right_norm
    own_left = jnp.ones((columns,), jnp.float32)
    own_right = jnp.ones((columns,), jnp.float32)
    own_inner = inner_mass
    for repeat in range(ITERS):
        rows_left, rows_right = lax.psum(
            (
                jnp.dot(own_left, tilted_left, precision=precise),
                jnp.dot(own_right, tilted_right, precision=precise),
            ),
            "rank",
        )
        row_scale_left = left_mass / rows_left
        row_scale_right = right_norm / rows_right
        col_total_left, col_total_right = lax.psum(
            (
                jnp.dot(tilted_left, row_scale_left, precision=precise),
                jnp.dot(tilted_right, row_scale_right, precision=precise),
            ),
            "rows",
        )
        own_inner, own_left, own_right = balance(
            own_inner, own_left, col_total_left, own_right, col_total_right
        )
    new_left = row_scale_left[None, :] * tilted_left * own_left[:, None]
    new_right = row_scale_right[None, :] * tilted_right * own_right[:, None]
    new_log_inner = jnp.log(own_inner) - jnp.log(total_left / RANK)
    return (new_left, new_right, new_log_inner)


def solution(mesh):
    in_specs = (
        P(None, "rows"),
        P(None, "rows"),
        P("rank", "rows"),
        P("rank", "rows"),
        P("rank"),
        P("rows"),
        P("rows"),
    )
    out_specs = (P("rank", "rows"), P("rank", "rows"), P("rank"))
    return jax.shard_map(
        per_device, mesh=mesh, in_specs=in_specs, out_specs=out_specs, check_vma=False
    )
```

profile of v0, /device:TPU:0, one launch (start us, length us, event | category | flops | bytes accessed | tf_op | source)
XLA Modules:
  0.0 222.6 jit_solution(15531989773435869686)
XLA Ops:
  0.6 0.0 copy-start
  0.6 0.0 copy-start.5
  0.7 1.4 reduce_sum.29
  2.1 0.0 copy-done.5
  2.1 0.6 reduce_sum.27
  2.7 0.0 copy-done
  2.7 0.0 copy-start.2
  2.7 0.0 copy-start.3
  2.7 1.4 fusion.2
  4.1 0.0 copy-done.2
  4.1 0.0 copy-done.3
  4.2 0.0 copy-start.1
  4.2 0.3 fusion
  4.5 40.8 %all-reduce.4 = (f32[128,64]{1,0:T(8,128)S(1)}, f32[]{:T(128)}) all-reduce(f32[128,64]{1,0:T(8,128)S(1)} %fusion, f32[]{:T(128)} %reduce_sum.27), channel_id=1, replica_groups=mesh['rows'=8,'rank'=4] {'rows'}, use_global_device_ids=true, to_apply=%region_2.0 | all-reduce | flops 8193 | bytes 65544 | tf_op jit(solution)/shard_map/psum | solution.py:37
  46.0 0.0 copy-start.6
  46.0 0.6 copy-done.6
  46.6 0.0 copy-done.1
  46.6 1.7 multiply_reduce_fusion
  48.3 34.9 %all-reduce.3 = (f32[128,64]{1,0:T(8,128)S(1)}, f32[64]{0:T(128)S(1)}, f32[]{:T(128)}) all-reduce(f32[128,64]{1,0:T(8,128)S(1)} %fusion.2, f32[64]{0:T(128)S(1)} %get-tuple-element.3, f32[]{:T(128)} %reduce_sum.29), channel_id=1, replica_groups=mesh['rows'=8,'rank'=4] {'rows'}, use_global_device_ids=true, to_apply=%region_4.0 | all-reduce | flops 8257 | bytes 66056 | tf_op jit(solution)/shard_map/psum | solution.py:37
  84.5 0.7 abs_reduce_fusion.2
  85.2 0.9 abs_reduce_fusion
  88.1 36.8 %pmax.7 = f32[]{:T(128)} all-reduce(f32[]{:T(128)S(6)} %max.12), channel_id=1, replica_groups=mesh['rows'=8,'rank'=4] {'rows','rank'}, use_global_device_ids=true, to_apply=%region_9.0 | all-reduce | flops 1 | bytes 8 | tf_op jit(solution)/shard_map/pmax | solution.py:57
  125.6 1.2 exponential_multiply_fusion
  126.8 0.4 fusion.16
  127.2 0.4 fusion.18
  127.5 0.0 copy-start.4
  127.5 11.1 %all-reduce.7 = (f32[2048]{0:T(1024)S(1)}, f32[2048]{0:T(1024)S(1)}) all-reduce(f32[2048]{0:T(1024)S(1)} %bitcast.64, f32[2048]{0:T(1024)S(1)} %bitcast.65), channel_id=1, replica_groups=mesh['rows'=8,'rank'=4] {'rank'}, use_global_device_ids=true, to_apply=%region_14.0 | all-reduce | flops 4096 | bytes 32768 | tf_op jit(solution)/shard_map/psum | solution.py:69
  138.7 0.0 copy-done.4
  138.7 0.5 convolution_bitcast_fusion.4
  139.2 0.5 convolution_bitcast_fusion.5
  139.7 20.3 %all-reduce.2 = (f32[64]{0:T(128)S(1)}, f32[64]{0:T(128)S(1)}) all-reduce(f32[64]{0:T(128)S(1)} %convolution_bitcast_fusion.4, f32[64]{0:T(128)S(1)} %convolution_bitcast_fusion.5), channel_id=1, replica_groups=mesh['rows'=8,'rank'=4] {'rows'}, use_global_device_ids=true, to_apply=%region_15.0 | all-reduce | flops 128 | bytes 1024 | tf_op jit(solution)/shard_map/psum | solution.py:78
  160.1 0.4 fusion.12
  160.5 0.4 fusion.14
  160.8 10.1 %all-reduce.6 = (f32[2048]{0:T(1024)S(1)}, f32[2048]{0:T(1024)S(1)}) all-reduce(f32[2048]{0:T(1024)S(1)} %bitcast.66, f32[2048]{0:T(1024)S(1)} %bitcast.67), channel_id=1, replica_groups=mesh['rows'=8,'rank'=4] {'rank'}, use_global_device_ids=true, to_apply=%region_18.0 | all-reduce | flops 4096 | bytes 32768 | tf_op jit(solution)/shard_map/psum | solution.py:69
  171.0 0.5 convolution_bitcast_fusion.2
  171.5 0.5 convolution_bitcast_fusion.3
  172.0 17.1 %all-reduce.1 = (f32[64]{0:T(128)S(1)}, f32[64]{0:T(128)S(1)}) all-reduce(f32[64]{0:T(128)S(1)} %convolution_bitcast_fusion.2, f32[64]{0:T(128)S(1)} %convolution_bitcast_fusion.3), channel_id=1, replica_groups=mesh['rows'=8,'rank'=4] {'rows'}, use_global_device_ids=true, to_apply=%region_19.0 | all-reduce | flops 128 | bytes 1024 | tf_op jit(solution)/shard_map/psum | solution.py:78
  189.2 0.4 fusion.8
  189.6 0.4 fusion.10
  189.9 10.1 %all-reduce.5 = (f32[2048]{0:T(1024)S(1)}, f32[2048]{0:T(1024)S(1)}) all-reduce(f32[2048]{0:T(1024)S(1)} %bitcast.68, f32[2048]{0:T(1024)S(1)} %bitcast.69), channel_id=1, replica_groups=mesh['rows'=8,'rank'=4] {'rank'}, use_global_device_ids=true, to_apply=%region_22.0 | all-reduce | flops 4096 | bytes 32768 | tf_op jit(solution)/shard_map/psum | solution.py:69
  200.1 0.5 convolution_bitcast_fusion
  200.6 0.5 convolution_bitcast_fusion.1
  201.1 19.1 %all-reduce = (f32[64]{0:T(128)S(1)}, f32[64]{0:T(128)S(1)}) all-reduce(f32[64]{0:T(128)S(1)} %convolution_bitcast_fusion, f32[64]{0:T(128)S(1)} %convolution_bitcast_fusion.1), channel_id=1, replica_groups=mesh['rows'=8,'rank'=4] {'rows'}, use_global_device_ids=true, to_apply=%region_23.0 | all-reduce | flops 128 | bytes 1024 | tf_op jit(solution)/shard_map/psum | solution.py:78
  220.3 0.5 log_subtract_fusion
  220.8 0.9 multiply_multiply_fusion.1
  221.7 0.9 multiply_multiply_fusion
  (12 shorter events, 0.1 us)
Async XLA Ops:
  0.6 2.1 copy-start
  0.6 1.5 copy-start.5
  2.7 1.4 copy-start.2
  2.7 1.4 copy-start.3
  4.2 42.5 %copy-start.1 = (f32[64,2048]{1,0:T(8,128)S(1)}, f32[64,2048]{1,0:T(8,128)}, u32[]{:S(2)}) copy-start(f32[64,2048]{1,0:T(8,128)} %param.9) | copy-start | bytes 1572868
  46.0 0.7 copy-start.6
  127.5 11.1 %copy-start.4 = (f32[2048]{0:T(1024)S(1)}, f32[2048]{0:T(1024)}, u32[]{:S(2)}) copy-start(f32[2048]{0:T(1024)} %param.13) | copy-start | bytes 24580
where the time goes:
time: 223 us
  blocking collectives  201 us (90%)
  matrix products  9.56 us (4%)
  other arithmetic  6.36 us (3%)
  between operations  5.5 us (2%)
    psum x2, blocking collectives, per_device(): lax.psum((contract_points(right_factor, right_round), contract_points(lef...  75.7 us
    psum x3, blocking collectives, per_device(): lax.psum((jnp.dot(tilted_left, row_scale_left, precision=precise), jnp.do...  56.6 us
    pmax x1, blocking collectives, per_device(): largest = lax.pmax(local_top, ('rows', 'rank'))  36.8 us
    psum x3, blocking collectives, per_device(): lax.psum((jnp.dot(own_left, tilted_left, precision=precise), jnp.dot(own_...  31.4 us

commit v1 on v0

v1 whole, which is shorter than its diff:
```python
import jax
import jax.numpy as jnp
from jax import lax
from jax.sharding import PartitionSpec as P

RANK = 256
ITERS = 3


def contract_points(factor, plan):
    return lax.dot_general(
        factor, plan, (((1,), (1,)), ((), ())), preferred_element_type=jnp.float32
    )


def expand_points(projected, factor):
    return lax.dot_general(
        projected, factor, (((0,), (0,)), ((), ())), preferred_element_type=jnp.float32
    )


def balance(inner_mass, col_scale_left, col_total_left, col_scale_right, col_total_right):
    mixed = (
        jnp.log(inner_mass)
        + jnp.log(col_scale_left * col_total_left)
        + jnp.log(col_scale_right * col_total_right)
    )
    inner_mass = jnp.exp(mixed / 3.0)
    return (inner_mass, inner_mass / col_total_left, inner_mass / col_total_right)


def solution(mesh):
    n_rows = mesh.shape["rows"]
    n_rank = mesh.shape["rank"]
    everyone = ("rows", "rank")
    n_all = n_rows * n_rank

    def sum_over_rows(value):
        if n_rows & (n_rows - 1):
            return lax.psum(value, "rows")
        stride = 1
        while stride < n_rows:
            pairs = [(i, i ^ stride) for i in range(n_rows)]
            value = value + lax.ppermute(value, "rows", pairs)
            stride *= 2
        return value

    def sum_over_rank(value):
        total = value
        for shift in range(1, n_rank):
            pairs = [(i, (i + shift) % n_rank) for i in range(n_rank)]
            total = total + lax.ppermute(value, "rank", pairs)
        return total

    def gather_everyone(value):
        spread = jnp.broadcast_to(value[None], (n_all,) + value.shape)
        got = lax.all_to_all(spread, everyone, 0, 0)
        return got.reshape(n_rows, n_rank, value.shape[-1])

    def per_device(left_factor, right_factor, left_plan, right_plan, log_inner, left_mass, right_mass):
        precise = lax.Precision.HIGHEST
        columns = left_plan.shape[0]
        depth = left_factor.shape[0]
        mine = lax.axis_index("rank")
        left_round = left_plan.astype(jnp.bfloat16)
        right_round = right_plan.astype(jnp.bfloat16)
        masses = jnp.stack([jnp.sum(left_mass), jnp.sum(right_mass)])
        masses = jnp.broadcast_to(masses[:, None], (2, columns))
        masses = jnp.concatenate([masses, jnp.zeros((6, columns), jnp.float32)])
        sums = sum_over_rows(
            jnp.concatenate(
                [
                    contract_points(right_factor, right_round),
                    contract_points(left_factor, left_round),
                    masses,
                ]
            )
        )
        proj_right = sums[:depth]
        proj_left = sums[depth : 2 * depth]
        total_left = sums[2 * depth, 0]
        total_right = sums[2 * depth + 1, 0]
        inner_mass = total_left / RANK * jnp.exp(log_inner)
        scaled_right = (proj_right / inner_mass[None, :]).astype(jnp.bfloat16)
        scaled_left = (proj_left / inner_mass[None, :]).astype(jnp.bfloat16)
        grad_left = expand_points(scaled_right, left_factor)
        grad_right = expand_points(scaled_left, right_factor)
        pairing = jnp.sum(scaled_right.astype(jnp.float32) * proj_left, axis=0)
        grad_inner = -pairing / inner_mass
        local_top = jnp.maximum(
            jnp.maximum(jnp.max(jnp.abs(grad_left)), jnp.max(jnp.abs(grad_right))),
            jnp.max(jnp.abs(grad_inner)),
        )
        largest = jnp.max(gather_everyone(jnp.full((1, 128), local_top)))
        step_size = 5.0 / jnp.maximum(largest, 0.25)
        tilted_left = left_plan * jnp.exp(-step_size * grad_left)
        tilted_right = right_plan * jnp.exp(-step_size * grad_right)
        inner_mass = inner_mass * jnp.exp(-step_size * grad_inner)
        right_norm = right_mass * (total_left / total_right)
        row_scale_left = left_mass
        row_scale_right = right_norm
        own_left = jnp.ones((columns,), jnp.float32)
        own_right = jnp.ones((columns,), jnp.float32)
        own_inner = inner_mass
        for repeat in range(ITERS):
            rows_both = sum_over_rank(
                jnp.stack(
                    [
                        jnp.dot(own_left, tilted_left, precision=precise),
                        jnp.dot(own_right, tilted_right, precision=precise),
                    ]
                )
            )
            row_scale_left = left_mass / rows_both[0]
            row_scale_right = right_norm / rows_both[1]
            partial = jnp.concatenate(
                [
                    jnp.dot(tilted_left, row_scale_left, precision=precise),
                    jnp.dot(tilted_right, row_scale_right, precision=precise),
                ]
            )
            parts = gather_everyone(partial[None])
            total = jnp.sum(lax.dynamic_index_in_dim(parts, mine, 1, False), axis=0)
            own_inner, own_left, own_right = balance(
                own_inner, own_left, total[:columns], own_right, total[columns:]
            )
        new_left = row_scale_left[None, :] * tilted_left * own_left[:, None]
        new_right = row_scale_right[None, :] * tilted_right * own_right[:, None]
        new_log_inner = jnp.log(own_inner) - jnp.log(total_left / RANK)
        return (new_left, new_right, new_log_inner)

    in_specs = (
        P(None, "rows"),
        P(None, "rows"),
        P("rank", "rows"),
        P("rank", "rows"),
        P("rank"),
        P("rows"),
        P("rows"),
    )
    out_specs = (P("rank", "rows"), P("rank", "rows"), P("rank"))
    return jax.shard_map(
        per_device, mesh=mesh, in_specs=in_specs, out_specs=out_specs, check_vma=False
    )
```

time: 223 us -> 96.5 us (0.43)
  blocking collectives: 201 us -> 23 us
  waiting for transfers between devices: 0 us -> 27.8 us
  starting transfers between devices: 0 us -> 18.4 us
  other arithmetic: 6.36 us -> 9.18 us
  local copies, waits for them, and re-layouts: 0.68 us -> 3.32 us
    psum x8 -> x0, blocking collectives: 164 us -> none  [the longest x2 75.7 us: per_device(): lax.psum((contract_points(right_factor, right_round), contract_points(lef...]
    pmax x1 -> x0, blocking collectives: 36.8 us -> none  [per_device(): largest = lax.pmax(local_top, ('rows', 'rank'))]
    all_to_all x0 -> x2, blocking collectives: none -> 23 us  [gather_everyone(): got = lax.all_to_all(spread, everyone, 0, 0)]
    all_to_all x0 -> x2, waiting for transfers between devices: none -> 14.2 us  [gather_everyone(): got = lax.all_to_all(spread, everyone, 0, 0)]
    ppermute x0 -> x12, waiting for transfers between devices: none -> 13.6 us  [the longest x3 8.15 us: sum_over_rows(): value = value + lax.ppermute(value, 'rows', pairs)]
    ppermute x0 -> x12, starting transfers between devices: none -> 13.3 us  [the longest x3 7.96 us: sum_over_rows(): value = value + lax.ppermute(value, 'rows', pairs)]
    all_to_all x0 -> x2, starting transfers between devices: none -> 5.09 us  [gather_everyone(): got = lax.all_to_all(spread, everyone, 0, 0)]
  transfers between devices with their start and end apart: 0 -> 14, of which waited for: 0 -> 10; matrix products, arithmetic and copies ran while one was open for 0% -> 0% of each run, Pallas kernels for 0% -> 0%
where the time goes in v1:
time: 96.5 us; the launch traced here: 96.1 us
  waiting for transfers between devices  27.8 us (29%)
  blocking collectives  23 us (24%)
  starting transfers between devices  18.4 us (19%)
  other arithmetic  9.18 us (10%)
  matrix products  8.95 us (9%)
  between operations  5.48 us (6%)
  local copies, waits for them, and re-layouts  3.32 us (3%)
    all_to_all x2, blocking collectives, gather_everyone(): got = lax.all_to_all(spread, everyone, 0, 0)  23 us
    all_to_all x2, waiting for transfers between devices, gather_everyone(): got = lax.all_to_all(spread, everyone, 0, 0)  14.2 us
    ppermute x3, waiting for transfers between devices, sum_over_rows(): value = value + lax.ppermute(value, 'rows', pairs)  8.15 us
    ppermute x3, starting transfers between devices, sum_over_rows(): value = value + lax.ppermute(value, 'rows', pairs)  7.96 us
    ppermute x9, waiting for transfers between devices, sum_over_rank(): total = total + lax.ppermute(value, 'rank', pairs)  5.46 us
    ppermute x9, starting transfers between devices, sum_over_rank(): total = total + lax.ppermute(value, 'rank', pairs)  5.37 us
    all_to_all x2, starting transfers between devices, gather_everyone(): got = lax.all_to_all(spread, everyone, 0, 0)  5.09 us
    reduce_sum x2, other arithmetic, per_device(): masses = jnp.stack([jnp.sum(left_mass), jnp.sum(right_mass)])  1.96 us
  transfers between devices with their start and end apart: 14, of which 10 were waited for; matrix products, arithmetic and copies ran while one was open for 0% of the time, Pallas kernels for 0%

profile of v1, /device:TPU:0, one launch (start us, length us, event | category | flops | bytes accessed | tf_op | source)
XLA Modules:
  0.0 96.1 jit_solution(13080323274443361457)
XLA Ops:
  0.7 1.4 %reduce_sum.54 = f32[]{:T(128)} reduce(f32[2048]{0:T(1024)} %param.12, f32[]{:T(128)} %constant.24.clone.1), dimensions={0}, to_apply=%region_0.0 | reduce | flops 2047 | bytes 8200 | tf_op jit(solution)/shard_map/reduce_sum | solution.py:67
  2.0 0.6 reduce_sum.55
  2.6 1.4 %fusion = f32[128,64]{0,1:T(8,128)S(1)} fusion(bf16[128,2048]{1,0:T(8,128)(2,1)S(1)} %copy-done, f32[64,2048]{1,0:T(8,128)} %param.9), kind=kOutput, calls=%fused_computation.12 | convolution fusion | flops 33685504 | bytes 1081344 | tf_op jit(solution)/shard_map/dot_general | solution.py:11
  4.4 1.4 %pad_maximum_fusion.3 = f32[264]{0:T(512)S(1)} fusion(f32[1]{0:T(128)} %bitcast.1, f32[1]{0:T(128)} %bitcast), kind=kLoop, calls=%fused_computation.32 | loop fusion | flops 264 | bytes 1064 | tf_op jit(solution)/shard_map/stack | solution.py:67
  5.9 3.1 %collective-permute-start = (f32[264,64]{0,1:T(8,128)S(1)}, f32[264,64]{0,1:T(8,128)S(1)}, u32[]{:S(2)}, u32[]{:S(2)}) collective-permute-start(f32[264,64]{0,1:T(8,128)S(1)} %maximum_maximum_fusion), channel_id=1, source_target_pairs={{0,4},{4,0},{8,12},{12,8},{16,20},{20,16},{24,28},{28,24},{1,5},{5... | collective-permute-start | bytes 202760 | tf_op jit(solution)/shard_map/ppermute | solution.py:44
  8.9 2.8 %collective-permute-done = f32[264,64]{0,1:T(8,128)S(1)} collective-permute-done((f32[264,64]{0,1:T(8,128)S(1)}, f32[264,64]{0,1:T(8,128)S(1)}, u32[]{:S(2)}, u32[]{:S(2)}) %collective-permute-start) | collective-permute-done | bytes 67616 | tf_op jit(solution)/shard_map/ppermute | solution.py:44
  11.7 1.9 %collective-permute-start.1 = (f32[264,64]{0,1:T(8,128)S(1)}, f32[264,64]{0,1:T(8,128)S(1)}, u32[]{:S(2)}, u32[]{:S(2)}) collective-permute-start(f32[264,64]{0,1:T(8,128)S(1)} %fusion.21), channel_id=1, source_target_pairs={{0,8},{4,12},{8,0},{12,4},{16,24},{20,28},{24,16},{28,20},{1,9},{5... | collective-permute-start | bytes 202760 | tf_op jit(solution)/shard_map/ppermute | solution.py:44
  13.7 2.7 %collective-permute-done.1 = f32[264,64]{0,1:T(8,128)S(1)} collective-permute-done((f32[264,64]{0,1:T(8,128)S(1)}, f32[264,64]{0,1:T(8,128)S(1)}, u32[]{:S(2)}, u32[]{:S(2)}) %collective-permute-start.1) | collective-permute-done | bytes 67616 | tf_op jit(solution)/shard_map/ppermute | solution.py:44
  16.4 3.0 %collective-permute-start.2 = (f32[264,64]{0,1:T(8,128)S(1)}, f32[264,64]{0,1:T(8,128)S(1)}, u32[]{:S(2)}, u32[]{:S(2)}) collective-permute-start(f32[264,64]{0,1:T(8,128)S(1)} %add.61), channel_id=1, source_target_pairs={{0,16},{4,20},{8,24},{12,28},{16,0},{20,4},{24,8},{28,12},{1,17},{... | collective-permute-start | bytes 202760 | tf_op jit(solution)/shard_map/ppermute | solution.py:44
  19.4 2.6 %collective-permute-done.2 = f32[264,64]{0,1:T(8,128)S(1)} collective-permute-done((f32[264,64]{0,1:T(8,128)S(1)}, f32[264,64]{0,1:T(8,128)S(1)}, u32[]{:S(2)}, u32[]{:S(2)}) %collective-permute-start.2) | collective-permute-done | bytes 67616 | tf_op jit(solution)/shard_map/ppermute | solution.py:44
  22.0 0.6 fusion.24
  23.3 0.6 copy-done.5
  23.9 0.9 abs_reduce_fusion.1
  24.8 0.9 abs_reduce_fusion
  26.0 0.6 abs_reduce_fusion.2
  28.5 14.1 %all_to_all.20 = f32[32,1,128]{2,1,0:T(1,128)S(1)} all-to-all(f32[32,1,128]{2,1,0:T(1,128)S(1)} %broadcast_in_dim_broadcast_in_dim_broadcast_in_dim.3), channel_id=1, replica_groups=mesh['rows'=8,'rank'=4] {'rows','rank'}, dimensions={0} | all-to-all | bytes 32768 | tf_op jit(solution)/shard_map/all_to_all | solution.py:57
  42.6 0.7 reduce_max.39
  43.9 1.2 %exponential_multiply_fusion = (f32[64,2048]{1,0:T(8,128)S(1)}, f32[64,2048]{1,0:T(8,128)S(1)}) fusion(f32[64,2048]{1,0:T(8,128)S(1)} %copy-done.2, f32[64,2048]{1,0:T(8,128)S(1)} %get-tuple-element.20, f32[]{:T(128)S(6)} %neg.9, f32[64,2048]{1,0:T(8,128)} %param.9, f32[64,2048]{1,0:T(8,128)S(1)} %get-tuple-element.18), kind=kLoop, calls=%fused_computation.8 | loop fusion | flops 524288 | bytes 3145732 | tf_op jit(solution)/shard_map/mul | solution.py:97
  45.9 0.6 collective-permute-start.4
  46.5 1.4 %collective-permute-start.5 = (f32[2,2048]{1,0:T(2,128)S(1)}, f32[2,2048]{1,0:T(2,128)S(1)}, u32[]{:S(2)}, u32[]{:S(2)}) collective-permute-start(f32[2,2048]{1,0:T(2,128)S(1)} %pad_maximum_fusion), channel_id=1, source_target_pairs={{0,3},{1,0},{2,1},{3,2},{4,7},{5,4},{6,5},{7,6},{8,11},{9,8},{10,9... | collective-permute-start | bytes 49160 | tf_op jit(solution)/shard_map/ppermute | solution.py:52
  49.2 0.5 collective-permute-done.4
  49.8 0.6 copy-done.3
  50.4 0.5 convolution_bitcast_fusion.5
  51.0 0.5 convolution_bitcast_fusion.4
  51.6 0.6 broadcast_in_dim.12
  52.2 2.5 %all-to-all-start.1 = ((f32[32,1,128]{2,1,0:T(1,128)}), f32[32,1,128]{2,1,0:T(1,128)S(1)}, u32[]{:S(2)}, u32[]{:S(2)}) async-start(f32[32,1,128]{2,1,0:T(1,128)} %broadcast_in_dim.12), calls=%async_computation.1 | async-start | bytes 32768 | tf_op jit(solution)/shard_map/all_to_all | solution.py:57
  54.7 7.1 %all-to-all-done.1 = f32[32,1,128]{2,1,0:T(1,128)S(1)} async-done(((f32[32,1,128]{2,1,0:T(1,128)}), f32[32,1,128]{2,1,0:T(1,128)S(1)}, u32[]{:S(2)}, u32[]{:S(2)}) %all-to-all-start.1) | async-done | bytes 16416 | tf_op jit(solution)/shard_map/all_to_all | solution.py:57
  62.3 0.4 fusion.11
  62.8 0.6 collective-permute-start.7
  63.4 1.4 %collective-permute-start.8 = (f32[2,2048]{1,0:T(2,128)S(1)}, f32[2,2048]{1,0:T(2,128)S(1)}, u32[]{:S(2)}, u32[]{:S(2)}) collective-permute-start(f32[2,2048]{1,0:T(2,128)S(1)} %pad_maximum_fusion.1), channel_id=1, source_target_pairs={{0,3},{1,0},{2,1},{3,2},{4,7},{5,4},{6,5},{7,6},{8,11},{9,8},{10,9... | collective-permute-start | bytes 49160 | tf_op jit(solution)/shard_map/ppermute | solution.py:52
  64.8 1.2 %collective-permute-done.6 = f32[2,2048]{1,0:T(2,128)S(1)} collective-permute-done((f32[2,2048]{1,0:T(2,128)S(1)}, f32[2,2048]{1,0:T(2,128)S(1)}, u32[]{:S(2)}, u32[]{:S(2)}) %collective-permute-start.6) | collective-permute-done | bytes 16416 | tf_op jit(solution)/shard_map/ppermute | solution.py:52
  66.0 0.7 collective-permute-done.7
  66.7 0.5 convolution_bitcast_fusion.3
  67.2 0.5 convolution_bitcast_fusion.2
  67.8 8.9 %all_to_all.21 = f32[32,1,128]{2,1,0:T(1,128)S(1)} all-to-all(f32[32,1,128]{2,1,0:T(1,128)S(1)} %broadcast_in_dim.13), channel_id=1, replica_groups=mesh['rows'=8,'rank'=4] {'rows','rank'}, dimensions={0} | all-to-all | bytes 32768 | tf_op jit(solution)/shard_map/all_to_all | solution.py:57
  77.2 0.4 fusion.7
  77.6 0.6 collective-permute-start.10
  78.2 0.7 collective-permute-start.11
  78.9 2.5 %collective-permute-done.10 = f32[2,2048]{1,0:T(2,128)S(1)} collective-permute-done((f32[2,2048]{1,0:T(2,128)S(1)}, f32[2,2048]{1,0:T(2,128)S(1)}, u32[]{:S(2)}, u32[]{:S(2)}) %collective-permute-start.10) | collective-permute-done | bytes 16416 | tf_op jit(solution)/shard_map/ppermute | solution.py:52
  81.4 0.6 collective-permute-done.9
  82.1 0.5 convolution_bitcast_fusion.1
  82.7 0.5 convolution_bitcast_fusion
  83.3 0.6 broadcast_in_dim.14
  83.9 2.5 %all-to-all-start.3 = ((f32[32,1,128]{2,1,0:T(1,128)}), f32[32,1,128]{2,1,0:T(1,128)S(1)}, u32[]{:S(2)}, u32[]{:S(2)}) async-start(f32[32,1,128]{2,1,0:T(1,128)} %broadcast_in_dim.14), calls=%async_computation.3 | async-start | bytes 32768 | tf_op jit(solution)/shard_map/all_to_all | solution.py:57
  86.5 7.1 %all-to-all-done.3 = f32[32,1,128]{2,1,0:T(1,128)S(1)} async-done(((f32[32,1,128]{2,1,0:T(1,128)}), f32[32,1,128]{2,1,0:T(1,128)S(1)}, u32[]{:S(2)}, u32[]{:S(2)}) %all-to-all-start.3) | async-done | bytes 16416 | tf_op jit(solution)/shard_map/all_to_all | solution.py:57
  93.6 0.6 log_subtract_fusion
  94.3 0.9 multiply_multiply_fusion
  95.2 0.9 multiply_multiply_fusion.1
  (59 shorter events, 3.0 us)
Async XLA Ops:
  0.6 2.0 %copy-start = (bf16[128,2048]{1,0:T(8,128)(2,1)S(1)}, bf16[128,2048]{1,0:T(8,128)(2,1)}, u32[]{:S(2)}) copy-start(bf16[128,2048]{1,0:T(8,128)(2,1)} %param.7) | copy-start | bytes 1572868
  0.6 1.4 %copy-start.4 = (f32[2048]{0:T(1024)S(1)}, f32[2048]{0:T(1024)}, u32[]{:S(2)}) copy-start(f32[2048]{0:T(1024)} %param.13) | copy-start | bytes 24580
  2.6 1.4 %copy-start.1 = (bf16[128,2048]{1,0:T(8,128)(2,1)S(1)}, bf16[128,2048]{1,0:T(8,128)(2,1)}, u32[]{:S(2)}) copy-start(bf16[128,2048]{1,0:T(8,128)(2,1)} %param.8) | copy-start | bytes 1572868
  2.6 1.4 %copy-start.2 = (f32[64,2048]{1,0:T(8,128)S(1)}, f32[64,2048]{1,0:T(8,128)}, u32[]{:S(2)}) copy-start(f32[64,2048]{1,0:T(8,128)} %param.10) | copy-start | bytes 1572868
  5.9 5.9 %collective-permute-start = (f32[264,64]{0,1:T(8,128)S(1)}, f32[264,64]{0,1:T(8,128)S(1)}, u32[]{:S(2)}, u32[]{:S(2)}) collective-permute-start(f32[264,64]{0,1:T(8,128)S(1)} %maximum_maximum_fusion), channel_id=1, source_target_pairs={{0,4},{4,0},{8,12},{12,8},{16,20},{20,16},{24,28},{28,24},{1,5},{5... | collective-permute-start | bytes 202760 | tf_op jit(solution)/shard_map/ppermute | solution.py:44
  11.7 4.7 %collective-permute-start.1 = (f32[264,64]{0,1:T(8,128)S(1)}, f32[264,64]{0,1:T(8,128)S(1)}, u32[]{:S(2)}, u32[]{:S(2)}) collective-permute-start(f32[264,64]{0,1:T(8,128)S(1)} %fusion.21), channel_id=1, source_target_pairs={{0,8},{4,12},{8,0},{12,4},{16,24},{20,28},{24,16},{28,20},{1,9},{5... | collective-permute-start | bytes 202760 | tf_op jit(solution)/shard_map/ppermute | solution.py:44
  16.4 5.6 %collective-permute-start.2 = (f32[264,64]{0,1:T(8,128)S(1)}, f32[264,64]{0,1:T(8,128)S(1)}, u32[]{:S(2)}, u32[]{:S(2)}) collective-permute-start(f32[264,64]{0,1:T(8,128)S(1)} %add.61), channel_id=1, source_target_pairs={{0,16},{4,20},{8,24},{12,28},{16,0},{20,4},{24,8},{28,12},{1,17},{... | collective-permute-start | bytes 202760 | tf_op jit(solution)/shard_map/ppermute | solution.py:44
  23.3 0.7 copy-start.5
  45.9 3.4 %collective-permute-start.3 = (f32[2,2048]{1,0:T(2,128)S(1)}, f32[2,2048]{1,0:T(2,128)S(1)}, u32[]{:S(2)}, u32[]{:S(2)}) collective-permute-start(f32[2,2048]{1,0:T(2,128)S(1)} %pad_maximum_fusion), channel_id=1, source_target_pairs={{0,1},{1,2},{2,3},{3,0},{4,5},{5,6},{6,7},{7,4},{8,9},{9,10},{10,1... | collective-permute-start | bytes 49160 | tf_op jit(solution)/shard_map/ppermute | solution.py:52
  45.9 3.8 %collective-permute-start.4 = (f32[2,2048]{1,0:T(2,128)S(1)}, f32[2,2048]{1,0:T(2,128)S(1)}, u32[]{:S(2)}, u32[]{:S(2)}) collective-permute-start(f32[2,2048]{1,0:T(2,128)S(1)} %pad_maximum_fusion), channel_id=1, source_target_pairs={{0,2},{1,3},{2,0},{3,1},{4,6},{5,7},{6,4},{7,5},{8,10},{9,11},{10,... | collective-permute-start | bytes 49160 | tf_op jit(solution)/shard_map/ppermute | solution.py:52
  46.5 3.2 %collective-permute-start.5 = (f32[2,2048]{1,0:T(2,128)S(1)}, f32[2,2048]{1,0:T(2,128)S(1)}, u32[]{:S(2)}, u32[]{:S(2)}) collective-permute-start(f32[2,2048]{1,0:T(2,128)S(1)} %pad_maximum_fusion), channel_id=1, source_target_pairs={{0,3},{1,0},{2,1},{3,2},{4,7},{5,4},{6,5},{7,6},{8,11},{9,8},{10,9... | collective-permute-start | bytes 49160 | tf_op jit(solution)/shard_map/ppermute | solution.py:52
  49.7 0.7 copy-start.3
  52.2 9.7 %all-to-all-start.1 = ((f32[32,1,128]{2,1,0:T(1,128)}), f32[32,1,128]{2,1,0:T(1,128)S(1)}, u32[]{:S(2)}, u32[]{:S(2)}) async-start(f32[32,1,128]{2,1,0:T(1,128)} %broadcast_in_dim.12), calls=%async_computation.1 | async-start | bytes 32768 | tf_op jit(solution)/shard_map/all_to_all | solution.py:57
  62.7 3.2 %collective-permute-start.6 = (f32[2,2048]{1,0:T(2,128)S(1)}, f32[2,2048]{1,0:T(2,128)S(1)}, u32[]{:S(2)}, u32[]{:S(2)}) collective-permute-start(f32[2,2048]{1,0:T(2,128)S(1)} %pad_maximum_fusion.1), channel_id=1, source_target_pairs={{0,1},{1,2},{2,3},{3,0},{4,5},{5,6},{6,7},{7,4},{8,9},{9,10},{10,1... | collective-permute-start | bytes 49160 | tf_op jit(solution)/shard_map/ppermute | solution.py:52
  62.8 3.8 %collective-permute-start.7 = (f32[2,2048]{1,0:T(2,128)S(1)}, f32[2,2048]{1,0:T(2,128)S(1)}, u32[]{:S(2)}, u32[]{:S(2)}) collective-permute-start(f32[2,2048]{1,0:T(2,128)S(1)} %pad_maximum_fusion.1), channel_id=1, source_target_pairs={{0,2},{1,3},{2,0},{3,1},{4,6},{5,7},{6,4},{7,5},{8,10},{9,11},{10,... | collective-permute-start | bytes 49160 | tf_op jit(solution)/shard_map/ppermute | solution.py:52
  63.4 3.2 %collective-permute-start.8 = (f32[2,2048]{1,0:T(2,128)S(1)}, f32[2,2048]{1,0:T(2,128)S(1)}, u32[]{:S(2)}, u32[]{:S(2)}) collective-permute-start(f32[2,2048]{1,0:T(2,128)S(1)} %pad_maximum_fusion.1), channel_id=1, source_target_pairs={{0,3},{1,0},{2,1},{3,2},{4,7},{5,4},{6,5},{7,6},{8,11},{9,8},{10,9... | collective-permute-start | bytes 49160 | tf_op jit(solution)/shard_map/ppermute | solution.py:52
  77.6 3.8 %collective-permute-start.10 = (f32[2,2048]{1,0:T(2,128)S(1)}, f32[2,2048]{1,0:T(2,128)S(1)}, u32[]{:S(2)}, u32[]{:S(2)}) collective-permute-start(f32[2,2048]{1,0:T(2,128)S(1)} %pad_maximum_fusion.2), channel_id=1, source_target_pairs={{0,2},{1,3},{2,0},{3,1},{4,6},{5,7},{6,4},{7,5},{8,10},{9,11},{10,... | collective-permute-start | bytes 49160 | tf_op jit(solution)/shard_map/ppermute | solution.py:52
  78.2 3.2 %collective-permute-start.11 = (f32[2,2048]{1,0:T(2,128)S(1)}, f32[2,2048]{1,0:T(2,128)S(1)}, u32[]{:S(2)}, u32[]{:S(2)}) collective-permute-start(f32[2,2048]{1,0:T(2,128)S(1)} %pad_maximum_fusion.2), channel_id=1, source_target_pairs={{0,3},{1,0},{2,1},{3,2},{4,7},{5,4},{6,5},{7,6},{8,11},{9,8},{10,9... | collective-permute-start | bytes 49160 | tf_op jit(solution)/shard_map/ppermute | solution.py:52
  78.9 3.2 %collective-permute-start.9 = (f32[2,2048]{1,0:T(2,128)S(1)}, f32[2,2048]{1,0:T(2,128)S(1)}, u32[]{:S(2)}, u32[]{:S(2)}) collective-permute-start(f32[2,2048]{1,0:T(2,128)S(1)} %pad_maximum_fusion.2), channel_id=1, source_target_pairs={{0,1},{1,2},{2,3},{3,0},{4,5},{5,6},{6,7},{7,4},{8,9},{9,10},{10,1... | collective-permute-start | bytes 49160 | tf_op jit(solution)/shard_map/ppermute | solution.py:52
  83.9 9.7 %all-to-all-start.3 = ((f32[32,1,128]{2,1,0:T(1,128)}), f32[32,1,128]{2,1,0:T(1,128)S(1)}, u32[]{:S(2)}, u32[]{:S(2)}) async-start(f32[32,1,128]{2,1,0:T(1,128)} %broadcast_in_dim.14), calls=%async_computation.3 | async-start | bytes 32768 | tf_op jit(solution)/shard_map/all_to_all | solution.py:57

commit v2 on v1

v2 whole, which is shorter than its diff:
```python
import functools

import jax
import jax.numpy as jnp
from jax import lax
from jax.experimental import pallas as pl
from jax.experimental.pallas import tpu as pltpu
from jax.sharding import PartitionSpec as P

RANK = 256
ITERS = 3
LANES = 128


def dot(a, b, a_dim, b_dim):
    return lax.dot_general(
        a, b, (((a_dim,), (b_dim,)), ((), ())), preferred_element_type=jnp.float32
    )


def call(body, out_shape, *args):
    specs = [pl.BlockSpec(memory_space=pltpu.SMEM)]
    specs += [pl.BlockSpec(memory_space=pltpu.VMEM) for _ in args[1:]]
    outs = jax.tree.map(lambda _: pl.BlockSpec(memory_space=pltpu.VMEM), out_shape)
    return pl.pallas_call(
        body,
        out_shape=out_shape,
        in_specs=specs,
        out_specs=outs,
        compiler_params=pltpu.CompilerParams(vmem_limit_bytes=32 * 2**20),
    )(*args)


def f32(*shape):
    return jax.ShapeDtypeStruct(shape, jnp.float32)


def project(n_rank, at, left_factor, right_factor, left_plan, right_plan, left_mass, right_mass, sums, *blocks):
    depth = left_factor.shape[0]
    columns = left_plan.shape[0]
    span = left_plan.shape[1] // n_rank
    sums[:depth, :columns] = dot(right_factor[...], right_plan[...].astype(jnp.bfloat16), 1, 1)
    sums[:depth, columns:] = dot(left_factor[...], left_plan[...].astype(jnp.bfloat16), 1, 1)
    sums[depth:, :columns] = jnp.full((8, columns), jnp.sum(left_mass[...]))
    sums[depth:, columns:] = jnp.full((8, columns), jnp.sum(right_mass[...]))
    for shift in range(n_rank):
        start = pl.multiple_of(((at[0] + shift) % n_rank) * span, LANES)
        blocks[shift][0] = left_plan[:, pl.ds(start, span)]
        blocks[shift][1] = right_plan[:, pl.ds(start, span)]


def gradients(at, sums, log_inner, left_factor, right_factor, scaled, grad_left, grad_right, top):
    depth = left_factor.shape[0]
    columns = log_inner.shape[1]
    total_left = sums[depth : depth + 1, :columns]
    inner = total_left / RANK * jnp.exp(log_inner[...])
    proj_left = sums[:depth, columns:]
    scaled_right = (sums[:depth, :columns] / inner).astype(jnp.bfloat16)
    scaled_left = (proj_left / inner).astype(jnp.bfloat16)
    up = dot(scaled_right, left_factor[...], 0, 0)
    grad_left[...] = up
    peak = jnp.max(jnp.abs(up))
    up = dot(scaled_left, right_factor[...], 0, 0)
    grad_right[...] = up
    peak = jnp.maximum(peak, jnp.max(jnp.abs(up)))
    right = scaled_right.astype(jnp.float32)
    pairing = jnp.sum(right * proj_left, axis=0, keepdims=True)
    grad_inner = -pairing / inner
    peak = jnp.maximum(peak, jnp.max(jnp.abs(grad_inner)))
    scaled[:depth, :columns] = right
    scaled[:depth, columns:] = scaled_left.astype(jnp.float32)
    scaled[depth:, :columns] = jnp.broadcast_to(inner, (8, columns))
    scaled[depth:, columns:] = jnp.broadcast_to(grad_inner, (8, columns))
    top[...] = jnp.full((1, LANES), peak)


def as_column(row):
    return jnp.broadcast_to(row, (LANES, row.shape[1])).T


def turn(n_rank, at, left_factor, right_factor, left_mass, right_mass, sums, *refs):
    scaled = refs[:n_rank]
    plans = refs[n_rank : 2 * n_rank]
    plan_out, grad_out, mass_out, inner_out = refs[2 * n_rank :]
    depth = left_factor.shape[0]
    columns = sums.shape[1] // 2
    span = left_factor.shape[1] // n_rank
    start = pl.multiple_of(at[0] * span, LANES)
    here = pl.ds(start, span)
    right = jnp.concatenate([s[:depth, :columns] for s in scaled], axis=1)
    left = jnp.concatenate([s[:depth, columns:] for s in scaled], axis=1)
    grad_out[0] = dot(left_factor[:, here], right.astype(jnp.bfloat16), 0, 0)
    grad_out[1] = dot(right_factor[:, here], left.astype(jnp.bfloat16), 0, 0)
    for side in range(2):
        plan_out[side] = jnp.concatenate([p[side].T for p in plans], axis=1)
    ratio = sums[depth : depth + 1, :1] / sums[depth : depth + 1, columns : columns + 1]
    mass_out[0] = as_column(left_mass[:, here])
    mass_out[1] = as_column(right_mass[:, here] * ratio)
    inner = jnp.concatenate([s[depth : depth + 1, :columns] for s in scaled], axis=1)
    grad_inner = jnp.concatenate([s[depth : depth + 1, columns:] for s in scaled], axis=1)
    inner_out[0:1] = inner
    inner_out[1:2] = grad_inner


def rolled(pair, shift):
    rows = jnp.concatenate([pair[0], pair[1]] * 4, axis=0)
    return pltpu.roll(rows, shift, 1)


def totals(n_rank, at, side_sum, all_k, columns):
    both = jnp.sum(side_sum[...], axis=0)
    half = all_k // LANES
    left = jnp.concatenate([both[i : i + 1] for i in range(half)], axis=1)
    right = jnp.concatenate([both[half + i : half + i + 1] for i in range(half)], axis=1)
    moved = rolled((left, right), ((n_rank - at[0]) % n_rank) * columns)
    return moved[0:1], moved[1:2]


def sweep(n_rank, at, columns, tilted, mass, scales, part, rows=None):
    got = []
    for side in range(2):
        block = tilted[side]
        weighted = block if scales is None else block * scales[side]
        row = mass[side] / jnp.sum(weighted, axis=1, keepdims=True)
        if rows is not None:
            rows[side] = row
        got.append(jnp.sum(block * row[:, :1], axis=0, keepdims=True))
    moved = rolled(got, at[0] * columns)
    half = moved.shape[1] // LANES
    for side in range(2):
        for i in range(half):
            part[side * half + i : side * half + i + 1] = moved[side : side + 1, i * LANES : (i + 1) * LANES]


def balance(inner, scales, sums):
    mixed = jnp.log(inner) + jnp.log(scales[0] * sums[0]) + jnp.log(scales[1] * sums[1])
    inner = jnp.exp(mixed / 3.0)
    return inner, (inner / sums[0], inner / sums[1])


def step_of(tops):
    return 5.0 / jnp.maximum(jnp.max(tops[...]), 0.25)


def tilt(n_rank, columns, at, tops, plan, grad, mass, inner_in, tilted, inner_out, part):
    step = step_of(tops)
    for side in range(2):
        tilted[side] = plan[side] * jnp.exp(-step * grad[side])
    inner_out[0:1] = inner_in[0:1] * jnp.exp(-step * inner_in[1:2])
    sweep(n_rank, at, columns, tilted, mass, None, part)


def again(n_rank, columns, first, at, parts, tilted, mass, state_in, state_out, part, rows):
    all_k = tilted.shape[2]
    sums = totals(n_rank, at, parts, all_k, columns)
    ones = jnp.ones((1, all_k), jnp.float32)
    old = (ones, ones) if first else (state_in[1:2], state_in[2:3])
    inner, scales = balance(state_in[0:1], old, sums)
    state_out[0:1] = inner
    state_out[1:2] = scales[0]
    state_out[2:3] = scales[1]
    sweep(n_rank, at, columns, tilted, mass, scales, part, rows)


def lay_rows(at, rows, flat):
    for side in range(2):
        flat[side : side + 1] = rows[side].T[0:1]


def own_points(n_rank, at, tops, left_plan, right_plan, grad_left, grad_right, *refs):
    flats = refs[:n_rank]
    left, right = refs[n_rank:]
    step = step_of(tops)
    span = left_plan.shape[1] // n_rank
    for shift in range(n_rank):
        start = pl.multiple_of(((at[0] + shift) % n_rank) * span, LANES)
        here = pl.ds(start, span)
        row = flats[shift]
        left[:, here] = row[0:1] * (left_plan[:, here] * jnp.exp(-step * grad_left[:, here]))
        right[:, here] = row[1:2] * (right_plan[:, here] * jnp.exp(-step * grad_right[:, here]))


def finish(n_rank, columns, at, parts, state, sums, left, right, new_left, new_right, new_log):
    all_k = state.shape[1]
    got = totals(n_rank, at, parts, all_k, columns)
    inner, scales = balance(state[0:1], (state[1:2], state[2:3]), got)
    depth = sums.shape[0] - 8
    new_log[...] = jnp.log(inner[:, :columns]) - jnp.log(sums[depth : depth + 1, :columns] / RANK)
    new_left[...] = left[...] * as_column(scales[0])[:columns, :1]
    new_right[...] = right[...] * as_column(scales[1])[:columns, :1]


def solution(mesh):
    n_rows = mesh.shape["rows"]
    n_rank = mesh.shape["rank"]
    everyone = ("rows", "rank")
    n_all = n_rows * n_rank

    def sum_over_rows(value):
        if n_rows & (n_rows - 1):
            return lax.psum(value, "rows")
        stride = 1
        while stride < n_rows:
            pairs = [(i, i ^ stride) for i in range(n_rows)]
            value = value + lax.ppermute(value, "rows", pairs)
            stride *= 2
        return value

    def to_everyone(value):
        spread = jnp.broadcast_to(value[None], (n_all,) + value.shape)
        return lax.all_to_all(spread, everyone, 0, 0)

    def from_rank(value, shift):
        return lax.ppermute(value, "rank", [((i + shift) % n_rank, i) for i in range(n_rank)])

    def per_device(left_factor, right_factor, left_plan, right_plan, log_inner, left_mass, right_mass):
        depth, points = left_factor.shape
        columns = left_plan.shape[0]
        all_k = columns * n_rank
        span = points // n_rank
        at = lax.axis_index("rank").reshape(1)
        left_mass = left_mass.reshape(1, points)
        right_mass = right_mass.reshape(1, points)

        sums, *blocks = call(
            functools.partial(project, n_rank),
            [f32(depth + 8, 2 * columns)] + [f32(2, columns, span)] * n_rank,
            at, left_factor, right_factor, left_plan, right_plan, left_mass, right_mass,
        )
        plans = [blocks[0]]
        for shift in range(1, n_rank):
            plans.append(
                lax.ppermute(blocks[shift], "rank", [(i, (i + shift) % n_rank) for i in range(n_rank)])
            )
        plans = [plans[(n_rank - s) % n_rank] for s in range(n_rank)]
        sums = sum_over_rows(sums)
        scaled, grad_left, grad_right, top = call(
            gradients,
            [f32(depth + 8, 2 * columns), f32(columns, points), f32(columns, points), f32(1, LANES)],
            at, sums, log_inner.reshape(1, columns), left_factor, right_factor,
        )
        tops = to_everyone(top)
        scaleds = [scaled] + [from_rank(scaled, s) for s in range(1, n_rank)]
        plan, grad, mass, inner = call(
            functools.partial(turn, n_rank),
            [f32(2, span, all_k), f32(2, span, all_k), f32(2, span, LANES), f32(8, all_k)],
            at, left_factor, right_factor, left_mass, right_mass, sums, *scaleds, *plans,
        )
        part_shape = f32(2 * all_k // LANES, LANES)
        tilted, state, part = call(
            functools.partial(tilt, n_rank, columns),
            [f32(2, span, all_k), f32(8, all_k), part_shape],
            at, tops, plan, grad, mass, inner,
        )
        for repeat in range(1, ITERS):
            parts = to_everyone(part)
            state, part, rows = call(
                functools.partial(again, n_rank, columns, repeat == 1),
                [f32(8, all_k), part_shape, f32(2, span, LANES)],
                at, parts, tilted, mass, state,
            )
        parts = to_everyone(part)
        flat = call(lay_rows, f32(2, span), at, rows)
        flats = [flat] + [from_rank(flat, s) for s in range(1, n_rank)]
        left, right = call(
            functools.partial(own_points, n_rank),
            [f32(columns, points)] * 2,
            at, tops, left_plan, right_plan, grad_left, grad_right, *flats,
        )
        new_left, new_right, new_log = call(
            functools.partial(finish, n_rank, columns),
            [f32(columns, points), f32(columns, points), f32(1, columns)],
            at, parts, state, sums, left, right,
        )
        return (new_left, new_right, new_log.reshape(columns))

    in_specs = (
        P(None, "rows"),
        P(None, "rows"),
        P("rank", "rows"),
        P("rank", "rows"),
        P("rank"),
        P("rows"),
        P("rows"),
    )
    out_specs = (P("rank", "rows"), P("rank", "rows"), P("rank"))
    return jax.shard_map(
        per_device, mesh=mesh, in_specs=in_specs, out_specs=out_specs, check_vma=False
    )
```

time: 96.5 us -> 86.4 us (0.90)
  local copies, waits for them, and re-layouts: 3.32 us -> 21.5 us
  waiting for transfers between devices: 27.8 us -> 11 us
  other arithmetic: 9.18 us -> 0.03 us
  matrix products: 8.95 us -> 0 us
  Pallas kernels: 0 us -> 7.68 us
  between operations: 5.48 us -> 0.78 us
  starting transfers between devices: 18.4 us -> 22.4 us
    unnamed x12 -> x60, local copies, waits for them, and re-layouts: 1.31 us -> 20.2 us
    all_to_all x2, waiting for transfers between devices: 14.2 us -> 2.11 us  [to_everyone(): return lax.all_to_all(spread, everyone, 0, 0)]
    dot_general x16 -> x0, matrix products: 8.95 us -> none  [the longest x2 1.86 us: expand_points(): lax.dot_general(projected, factor, (((0,), (0,)), ((), ())), preferred_el...]
    pallas_call x0 -> x9, Pallas kernels: none -> 7.68 us  [call(): pl.pallas_call(body, out_shape=out_shape, in_specs=specs, out_specs=outs,...]
    ppermute x9, waiting for transfers between devices: 5.46 us -> 1.34 us  [the longest x6 1.34 us: from_rank(): lax.ppermute(value, 'rank', [((i + shift) % n_rank, i) for i in range(n_r...]
    all_to_all x2, starting transfers between devices: 5.09 us -> 9.08 us  [to_everyone(): return lax.all_to_all(spread, everyone, 0, 0)]
    mul x4 -> x0, other arithmetic: 2.99 us -> none  [the longest x1 1.19 us: per_device(): tilted_right = right_plan * jnp.exp(-step_size * grad_right)]
    reduce_sum x6 -> x0, other arithmetic: 2.19 us -> none  [the longest x2 1.96 us: per_device(): masses = jnp.stack([jnp.sum(left_mass), jnp.sum(right_mass)])]
  transfers between devices with their start and end apart: 14 -> 14, of which waited for: 10 -> 6; matrix products, arithmetic and copies ran while one was open for 0% -> 1% of each run, Pallas kernels for 0% -> 3%
where the time goes in v2:
time: 86.4 us; the launch traced here: 85.5 us
  starting transfers between devices  22.4 us (26%)
  blocking collectives  22.2 us (26%)
  local copies, waits for them, and re-layouts  21.5 us (25%)
  waiting for transfers between devices  11 us (13%)
  Pallas kernels  7.68 us (9%)
    all_to_all x2, blocking collectives, to_everyone(): return lax.all_to_all(spread, everyone, 0, 0)  22.2 us
    unnamed x60, local copies, waits for them, and re-layouts  20.2 us
    all_to_all x2, starting transfers between devices, to_everyone(): return lax.all_to_all(spread, everyone, 0, 0)  9.08 us
    pallas_call x9, Pallas kernels, call(): pl.pallas_call(body, out_shape=out_shape, in_specs=specs, out_specs=outs,...  7.68 us
    ppermute x3, waiting for transfers between devices, sum_over_rows(): value = value + lax.ppermute(value, 'rows', pairs)  7.57 us
    ppermute x3, starting transfers between devices, sum_over_rows(): value = value + lax.ppermute(value, 'rows', pairs)  5.82 us
    ppermute x6, starting transfers between devices, from_rank(): lax.ppermute(value, 'rank', [((i + shift) % n_rank, i) for i in range(n_r...  4.51 us
    ppermute x3, starting transfers between devices, per_device(): lax.ppermute(blocks[shift], 'rank', [(i, (i + shift) % n_rank) for i in r...  2.97 us
  transfers between devices with their start and end apart: 14, of which 6 were waited for; matrix products, arithmetic and copies ran while one was open for 1% of the time, Pallas kernels for 3%

profile of v2, /device:TPU:0, one launch (start us, length us, event | category | flops | bytes accessed | tf_op | source)
XLA Modules:
  0.0 85.5 jit_solution(15821825605303688734)
XLA Ops:
  0.6 0.7 copy-done.26
  1.3 1.0 %copy-done = bf16[128,2048]{1,0:T(8,128)(2,1)S(1)} copy-done((bf16[128,2048]{1,0:T(8,128)(2,1)S(1)}, bf16[128,2048]{1,0:T(8,128)(2,1)}, u32[]{:S(2)}) %copy-start) | copy-done | bytes 524312
  2.4 1.0 %copy-done.2 = bf16[128,2048]{1,0:T(8,128)(2,1)S(1)} copy-done((bf16[128,2048]{1,0:T(8,128)(2,1)S(1)}, bf16[128,2048]{1,0:T(8,128)(2,1)}, u32[]{:S(2)}) %copy-start.2) | copy-done | bytes 524312
  3.4 1.0 %copy-done.4 = f32[64,2048]{1,0:T(8,128)S(1)} copy-done((f32[64,2048]{1,0:T(8,128)S(1)}, f32[64,2048]{1,0:T(8,128)}, u32[]{:S(2)}) %copy-start.4) | copy-done | bytes 524312
  4.5 1.0 %copy-done.6 = f32[64,2048]{1,0:T(8,128)S(1)} copy-done((f32[64,2048]{1,0:T(8,128)S(1)}, f32[64,2048]{1,0:T(8,128)}, u32[]{:S(2)}) %copy-start.6) | copy-done | bytes 524312
  5.5 0.7 copy-done.27
  6.2 1.2 %shard_map.94 = (f32[136,128]{1,0:T(8,128)S(1)}, f32[2,64,512]{2,1,0:T(8,128)S(1)}, f32[2,64,512]{2,1,0:T(8,128)}, f32[2,64,512]{2,1,0:T(8,128)}, f32[2,64,512]{2,1,0:T(8,128)S(1)}) custom-call(s32[1]{0:T(128)} %bitcast.at, bf16[128,2048]{1,0:T(8,128)(2,1)S(1)} %copy-done, bf16[128,2048]{1,0:T(8,128)(2,1)S(1)} %copy-done.2, f32[64,2048]{1,0:T(8,128)S(1)} %copy-done.4, ...), custom_call_target="tpu_custom_call" | custom-call | tf_op jit(solution)/shard_map/pallas_call | solution.py:25
  7.4 2.4 %collective-permute-start.6 = (f32[2,64,512]{2,1,0:T(8,128)S(1)}, f32[2,64,512]{2,1,0:T(8,128)S(1)}, u32[]{:S(2)}, u32[]{:S(2)}) collective-permute-start(f32[2,64,512]{2,1,0:T(8,128)S(1)} %get-tuple-element.33), channel_id=1, source_target_pairs={{0,3},{1,0},{2,1},{3,2},{4,7},{5,4},{6,5},{7,6},{8,11},{9,8},{10,9... | collective-permute-start | bytes 786440 | tf_op jit(solution)/shard_map/ppermute | solution.py:233
  9.8 1.5 %collective-permute-start = (f32[136,128]{1,0:T(8,128)S(1)}, f32[136,128]{1,0:T(8,128)S(1)}, u32[]{:S(2)}, u32[]{:S(2)}) collective-permute-start(f32[136,128]{1,0:T(8,128)S(1)} %get-tuple-element.29), channel_id=1, source_target_pairs={{0,4},{4,0},{8,12},{12,8},{16,20},{20,16},{24,28},{28,24},{1,5},{5... | collective-permute-start | bytes 208904 | tf_op jit(solution)/shard_map/ppermute | solution.py:205
  11.9 2.2 %collective-permute-done = f32[136,128]{1,0:T(8,128)S(1)} collective-permute-done((f32[136,128]{1,0:T(8,128)S(1)}, f32[136,128]{1,0:T(8,128)S(1)}, u32[]{:S(2)}, u32[]{:S(2)}) %collective-permute-start) | collective-permute-done | bytes 69664 | tf_op jit(solution)/shard_map/ppermute | solution.py:205
  14.2 1.6 %collective-permute-start.1 = (f32[136,128]{1,0:T(8,128)S(1)}, f32[136,128]{1,0:T(8,128)S(1)}, u32[]{:S(2)}, u32[]{:S(2)}) collective-permute-start(f32[136,128]{1,0:T(8,128)S(1)} %add.9), channel_id=1, source_target_pairs={{0,8},{4,12},{8,0},{12,4},{16,24},{20,28},{24,16},{28,20},{1,9},{5... | collective-permute-start | bytes 208904 | tf_op jit(solution)/shard_map/ppermute | solution.py:205
  15.8 2.7 %collective-permute-done.1 = f32[136,128]{1,0:T(8,128)S(1)} collective-permute-done((f32[136,128]{1,0:T(8,128)S(1)}, f32[136,128]{1,0:T(8,128)S(1)}, u32[]{:S(2)}, u32[]{:S(2)}) %collective-permute-start.1) | collective-permute-done | bytes 69664 | tf_op jit(solution)/shard_map/ppermute | solution.py:205
  18.5 2.7 %collective-permute-start.2 = (f32[136,128]{1,0:T(8,128)S(1)}, f32[136,128]{1,0:T(8,128)S(1)}, u32[]{:S(2)}, u32[]{:S(2)}) collective-permute-start(f32[136,128]{1,0:T(8,128)S(1)} %add.10), channel_id=1, source_target_pairs={{0,16},{4,20},{8,24},{12,28},{16,0},{20,4},{24,8},{28,12},{1,17},{... | collective-permute-start | bytes 208904 | tf_op jit(solution)/shard_map/ppermute | solution.py:205
  21.2 2.6 %collective-permute-done.2 = f32[136,128]{1,0:T(8,128)S(1)} collective-permute-done((f32[136,128]{1,0:T(8,128)S(1)}, f32[136,128]{1,0:T(8,128)S(1)}, u32[]{:S(2)}, u32[]{:S(2)}) %collective-permute-start.2) | collective-permute-done | bytes 69664 | tf_op jit(solution)/shard_map/ppermute | solution.py:205
  23.8 0.6 copy-done.29
  25.1 0.8 copy-done.10
  25.9 0.8 collective-permute-start.4
  26.7 0.7 copy-done.12
  27.7 0.6 copy-done.18
  28.3 0.6 broadcast_in_dim.11
  28.9 6.5 %all-to-all-start = ((f32[32,1,128]{2,1,0:T(1,128)}), f32[32,1,128]{2,1,0:T(1,128)S(1)}, u32[]{:S(2)}, u32[]{:S(2)}) async-start(f32[32,1,128]{2,1,0:T(1,128)} %broadcast_in_dim.11), calls=%async_computation | async-start | bytes 32768 | tf_op jit(solution)/shard_map/all_to_all | solution.py:211
  35.4 0.7 copy-done.14
  36.1 0.7 copy-done.16
  36.8 0.6 copy-done.20
  37.5 0.6 copy-done.22
  38.1 0.6 copy-done.24
  38.7 0.9 %copy-done.13 = f32[2,64,512]{2,1,0:T(8,128)S(1)} copy-done((f32[2,64,512]{2,1,0:T(8,128)S(1)}, f32[2,64,512]{2,1,0:T(8,128)}, u32[]{:S(2)}) %copy-start.13) | copy-done | bytes 262168
  39.7 0.9 %copy-done.15 = f32[2,64,512]{2,1,0:T(8,128)S(1)} copy-done((f32[2,64,512]{2,1,0:T(8,128)S(1)}, f32[2,64,512]{2,1,0:T(8,128)}, u32[]{:S(2)}) %copy-start.15) | copy-done | bytes 262168
  40.6 0.9 %copy-done.17 = f32[2,64,512]{2,1,0:T(8,128)S(1)} copy-done((f32[2,64,512]{2,1,0:T(8,128)S(1)}, f32[2,64,512]{2,1,0:T(8,128)}, u32[]{:S(2)}) %copy-start.17) | copy-done | bytes 262168
  41.6 0.9 %copy-done.19 = f32[136,128]{1,0:T(8,128)S(1)} copy-done((f32[136,128]{1,0:T(8,128)S(1)}, f32[136,128]{1,0:T(8,128)}, u32[]{:S(2)}) %copy-start.19) | copy-done | bytes 69656
  42.5 0.9 %copy-done.21 = f32[136,128]{1,0:T(8,128)S(1)} copy-done((f32[136,128]{1,0:T(8,128)S(1)}, f32[136,128]{1,0:T(8,128)}, u32[]{:S(2)}) %copy-start.21) | copy-done | bytes 69656
  43.3 0.9 %copy-done.23 = f32[136,128]{1,0:T(8,128)S(1)} copy-done((f32[136,128]{1,0:T(8,128)S(1)}, f32[136,128]{1,0:T(8,128)}, u32[]{:S(2)}) %copy-start.23) | copy-done | bytes 69656
  44.2 0.9 %copy-done.25 = f32[136,128]{1,0:T(8,128)S(1)} copy-done((f32[136,128]{1,0:T(8,128)S(1)}, f32[136,128]{1,0:T(8,128)}, u32[]{:S(2)}) %copy-start.25) | copy-done | bytes 69656
  45.1 1.6 %shard_map.96 = (f32[2,512,256]{2,1,0:T(8,128)S(1)}, f32[2,512,256]{2,1,0:T(8,128)S(1)}, f32[2,512,128]{2,1,0:T(8,128)S(1)}, f32[8,256]{1,0:T(8,128)S(1)}) custom-call(s32[1]{0:T(128)} %bitcast.at, bf16[128,2048]{1,0:T(8,128)(2,1)S(1)} %copy-done.1, bf16[128,2048]{1,0:T(8,128)(2,1)S(1)} %copy-done.3, f32[1,2048]{1,0:T(1,128)S(1)} %bitcast.7, ...), custom_call_target="tpu_custom_call" | custom-call | tf_op jit(solution)/shard_map/pallas_call | solution.py:25
  46.7 1.0 %copy-done.8 = f32[2,512,256]{2,1,0:T(8,128)} copy-done((f32[2,512,256]{2,1,0:T(8,128)}, f32[2,512,256]{2,1,0:T(8,128)S(1)}, u32[]{:S(2)}) %copy-start.8) | copy-done | bytes 1048600
  47.7 1.2 %copy-done.9 = f32[2,512,256]{2,1,0:T(8,128)S(1)} copy-done((f32[2,512,256]{2,1,0:T(8,128)S(1)}, f32[2,512,256]{2,1,0:T(8,128)}, u32[]{:S(2)}) %copy-start.9) | copy-done | bytes 1048600
  48.9 0.7 shard_map.97
  49.6 13.0 %all_to_all.20.parts = f32[32,4,128]{2,1,0:T(4,128)S(1)} all-to-all(f32[32,4,128]{2,1,0:T(4,128)S(1)} %broadcast_in_dim.12), channel_id=1, replica_groups=mesh['rows'=8,'rank'=4] {'rows','rank'}, dimensions={0} | all-to-all | bytes 131072 | tf_op jit(solution)/shard_map/all_to_all | solution.py:211
  62.7 1.2 %shard_map.98 = (f32[8,256]{1,0:T(8,128)S(1)}, f32[4,128]{1,0:T(4,128)S(1)}, f32[2,512,128]{2,1,0:T(8,128)}) custom-call(s32[1]{0:T(128)} %bitcast.at, f32[32,4,128]{2,1,0:T(4,128)S(1)} %all_to_all.20.parts, f32[2,512,256]{2,1,0:T(8,128)S(1)} %get-tuple-element.41.tilted, f32[2,512,128]{2,1,0:T(8,128)S(1)} %get-tuple-element.38.mass, ...), custom_call_target="tpu_custom_call" | custom-call | tf_op jit(solution)/shard_map/pallas_call | solution.py:25
  63.8 9.1 %all_to_all.21.parts = f32[32,4,128]{2,1,0:T(4,128)S(1)} all-to-all(f32[32,4,128]{2,1,0:T(4,128)S(1)} %broadcast_in_dim.13), channel_id=1, replica_groups=mesh['rows'=8,'rank'=4] {'rows','rank'}, dimensions={0} | all-to-all | bytes 131072 | tf_op jit(solution)/shard_map/all_to_all | solution.py:211
  73.0 0.6 shard_map.99
  73.6 0.6 broadcast_in_dim.14
  74.2 2.6 %all-to-all-start.3 = ((f32[32,4,128]{2,1,0:T(4,128)}), f32[32,4,128]{2,1,0:T(4,128)S(1)}, u32[]{:S(2)}, u32[]{:S(2)}) async-start(f32[32,4,128]{2,1,0:T(4,128)} %broadcast_in_dim.14), calls=%async_computation.3 | async-start | bytes 131072 | tf_op jit(solution)/shard_map/all_to_all | solution.py:211
  77.0 1.7 %collective-permute-start.10 = (f32[2,512]{1,0:T(2,128)S(1)}, f32[2,512]{1,0:T(2,128)S(1)}, u32[]{:S(2)}, u32[]{:S(2)}) collective-permute-start(f32[2,512]{1,0:T(2,128)S(1)} %shard_map.100.refs_0_), channel_id=1, source_target_pairs={{2,0},{3,1},{0,2},{1,3},{6,4},{7,5},{4,6},{5,7},{10,8},{11,9},{8,1... | collective-permute-start | bytes 12296 | tf_op jit(solution)/shard_map/ppermute | solution.py:214
  78.6 1.7 %collective-permute-start.9 = (f32[2,512]{1,0:T(2,128)S(1)}, f32[2,512]{1,0:T(2,128)S(1)}, u32[]{:S(2)}, u32[]{:S(2)}) collective-permute-start(f32[2,512]{1,0:T(2,128)S(1)} %shard_map.100.refs_0_), channel_id=1, source_target_pairs={{1,0},{2,1},{3,2},{0,3},{5,4},{6,5},{7,6},{4,7},{9,8},{10,9},{11,1... | collective-permute-start | bytes 12296 | tf_op jit(solution)/shard_map/ppermute | solution.py:214
  80.6 1.1 %collective-permute-done.11.refs_3_ = f32[2,512]{1,0:T(2,128)S(1)} collective-permute-done((f32[2,512]{1,0:T(2,128)S(1)}, f32[2,512]{1,0:T(2,128)S(1)}, u32[]{:S(2)}, u32[]{:S(2)}) %collective-permute-start.11) | collective-permute-done | bytes 4128 | tf_op jit(solution)/shard_map/ppermute | solution.py:214
  82.1 2.1 %all-to-all-done.3.parts = f32[32,4,128]{2,1,0:T(4,128)S(1)} async-done(((f32[32,4,128]{2,1,0:T(4,128)}), f32[32,4,128]{2,1,0:T(4,128)S(1)}, u32[]{:S(2)}, u32[]{:S(2)}) %all-to-all-start.3) | async-done | bytes 65568 | tf_op jit(solution)/shard_map/all_to_all | solution.py:211
  84.2 1.3 %shard_map.102 = (f32[64,2048]{1,0:T(8,128)}, f32[64,2048]{1,0:T(8,128)}, f32[1,64]{1,0:T(1,128)}) custom-call(s32[1]{0:T(128)} %bitcast.at, f32[32,4,128]{2,1,0:T(4,128)S(1)} %all-to-all-done.3.parts, f32[8,256]{1,0:T(8,128)S(1)} %get-tuple-element.46.state, f32[136,128]{1,0:T(8,128)S(1)} %add.11.sums, f32[64,2048]{1,0:T(8,128)S(1)} %get-tuple-element.50.left, ...), custom_call_target="tpu_custom_call" | custom-call | tf_op jit(solution)/shard_map/pallas_call | solution.py:25
  (58 shorter events, 2.3 us)
Async XLA Ops:
  0.6 0.7 copy-start.26
  1.3 1.0 %copy-start = (bf16[128,2048]{1,0:T(8,128)(2,1)S(1)}, bf16[128,2048]{1,0:T(8,128)(2,1)}, u32[]{:S(2)}) copy-start(bf16[128,2048]{1,0:T(8,128)(2,1)} %left_factor.5) | copy-start | bytes 1572868
  2.4 1.0 %copy-start.2 = (bf16[128,2048]{1,0:T(8,128)(2,1)S(1)}, bf16[128,2048]{1,0:T(8,128)(2,1)}, u32[]{:S(2)}) copy-start(bf16[128,2048]{1,0:T(8,128)(2,1)} %right_factor.5) | copy-start | bytes 1572868
  3.4 1.0 %copy-start.4 = (f32[64,2048]{1,0:T(8,128)S(1)}, f32[64,2048]{1,0:T(8,128)}, u32[]{:S(2)}) copy-start(f32[64,2048]{1,0:T(8,128)} %left_plan.3) | copy-start | bytes 1572868
  4.5 1.0 %copy-start.6 = (f32[64,2048]{1,0:T(8,128)S(1)}, f32[64,2048]{1,0:T(8,128)}, u32[]{:S(2)}) copy-start(f32[64,2048]{1,0:T(8,128)} %right_plan.3) | copy-start | bytes 1572868
  5.5 0.7 copy-start.27
  7.4 19.3 %collective-permute-start.6 = (f32[2,64,512]{2,1,0:T(8,128)S(1)}, f32[2,64,512]{2,1,0:T(8,128)S(1)}, u32[]{:S(2)}, u32[]{:S(2)}) collective-permute-start(f32[2,64,512]{2,1,0:T(8,128)S(1)} %get-tuple-element.33), channel_id=1, source_target_pairs={{0,3},{1,0},{2,1},{3,2},{4,7},{5,4},{6,5},{7,6},{8,11},{9,8},{10,9... | collective-permute-start | bytes 786440 | tf_op jit(solution)/shard_map/ppermute | solution.py:233
  9.8 4.3 %collective-permute-start = (f32[136,128]{1,0:T(8,128)S(1)}, f32[136,128]{1,0:T(8,128)S(1)}, u32[]{:S(2)}, u32[]{:S(2)}) collective-permute-start(f32[136,128]{1,0:T(8,128)S(1)} %get-tuple-element.29), channel_id=1, source_target_pairs={{0,4},{4,0},{8,12},{12,8},{16,20},{20,16},{24,28},{28,24},{1,5},{5... | collective-permute-start | bytes 208904 | tf_op jit(solution)/shard_map/ppermute | solution.py:205
  11.4 24.1 %collective-permute-start.7 = (f32[2,64,512]{2,1,0:T(8,128)}, f32[2,64,512]{2,1,0:T(8,128)S(1)}, u32[]{:S(2)}, u32[]{:S(2)}) collective-permute-start(f32[2,64,512]{2,1,0:T(8,128)} %get-tuple-element.34), channel_id=1, source_target_pairs={{0,2},{1,3},{2,0},{3,1},{4,6},{5,7},{6,4},{7,5},{8,10},{9,11},{10,... | collective-permute-start | bytes 786440 | tf_op jit(solution)/shard_map/ppermute | solution.py:233
  11.9 24.2 %collective-permute-start.8 = (f32[2,64,512]{2,1,0:T(8,128)}, f32[2,64,512]{2,1,0:T(8,128)S(1)}, u32[]{:S(2)}, u32[]{:S(2)}) collective-permute-start(f32[2,64,512]{2,1,0:T(8,128)} %get-tuple-element.35), channel_id=1, source_target_pairs={{0,1},{1,2},{2,3},{3,0},{4,5},{5,6},{6,7},{7,4},{8,9},{9,10},{10,1... | collective-permute-start | bytes 786440 | tf_op jit(solution)/shard_map/ppermute | solution.py:233
  14.2 4.4 %collective-permute-start.1 = (f32[136,128]{1,0:T(8,128)S(1)}, f32[136,128]{1,0:T(8,128)S(1)}, u32[]{:S(2)}, u32[]{:S(2)}) collective-permute-start(f32[136,128]{1,0:T(8,128)S(1)} %add.9), channel_id=1, source_target_pairs={{0,8},{4,12},{8,0},{12,4},{16,24},{20,28},{24,16},{28,20},{1,9},{5... | collective-permute-start | bytes 208904 | tf_op jit(solution)/shard_map/ppermute | solution.py:205
  18.5 5.3 %collective-permute-start.2 = (f32[136,128]{1,0:T(8,128)S(1)}, f32[136,128]{1,0:T(8,128)S(1)}, u32[]{:S(2)}, u32[]{:S(2)}) collective-permute-start(f32[136,128]{1,0:T(8,128)S(1)} %add.10), channel_id=1, source_target_pairs={{0,16},{4,20},{8,24},{12,28},{16,0},{20,4},{24,8},{28,12},{1,17},{... | collective-permute-start | bytes 208904 | tf_op jit(solution)/shard_map/ppermute | solution.py:205
  23.8 0.7 copy-start.29
  24.5 14.2 %copy-start.1 = (bf16[128,2048]{1,0:T(8,128)(2,1)S(1)}, bf16[128,2048]{1,0:T(8,128)(2,1)}, u32[]{:S(2)}) copy-start(bf16[128,2048]{1,0:T(8,128)(2,1)} %left_factor.5) | copy-start | bytes 1572868
  24.5 14.2 %copy-start.3 = (bf16[128,2048]{1,0:T(8,128)(2,1)S(1)}, bf16[128,2048]{1,0:T(8,128)(2,1)}, u32[]{:S(2)}) copy-start(bf16[128,2048]{1,0:T(8,128)(2,1)} %right_factor.5) | copy-start | bytes 1572868
  25.1 0.8 copy-start.10
  25.9 11.0 %collective-permute-start.3 = (f32[136,128]{1,0:T(8,128)S(1)}, f32[136,128]{1,0:T(8,128)S(1)}, u32[]{:S(2)}, u32[]{:S(2)}) collective-permute-start(f32[136,128]{1,0:T(8,128)S(1)} %get-tuple-element.31.refs_0_), channel_id=1, source_target_pairs={{1,0},{2,1},{3,2},{0,3},{5,4},{6,5},{7,6},{4,7},{9,8},{10,9},{11,1... | collective-permute-start | bytes 208904 | tf_op jit(solution)/shard_map/ppermute | solution.py:214
  25.9 11.6 %collective-permute-start.4 = (f32[136,128]{1,0:T(8,128)S(1)}, f32[136,128]{1,0:T(8,128)S(1)}, u32[]{:S(2)}, u32[]{:S(2)}) collective-permute-start(f32[136,128]{1,0:T(8,128)S(1)} %get-tuple-element.31.refs_0_), channel_id=1, source_target_pairs={{2,0},{3,1},{0,2},{1,3},{6,4},{7,5},{4,6},{5,7},{10,8},{11,9},{8,1... | collective-permute-start | bytes 208904 | tf_op jit(solution)/shard_map/ppermute | solution.py:214
  26.7 0.7 copy-start.12
  27.4 10.7 %collective-permute-start.5 = (f32[136,128]{1,0:T(8,128)S(1)}, f32[136,128]{1,0:T(8,128)S(1)}, u32[]{:S(2)}, u32[]{:S(2)}) collective-permute-start(f32[136,128]{1,0:T(8,128)S(1)} %get-tuple-element.31.refs_0_), channel_id=1, source_target_pairs={{3,0},{0,1},{1,2},{2,3},{7,4},{4,5},{5,6},{6,7},{11,8},{8,9},{9,10... | collective-permute-start | bytes 208904 | tf_op jit(solution)/shard_map/ppermute | solution.py:214
  27.7 0.6 copy-start.18
  28.9 9.8 %copy-start.28 = (f32[2048]{0:T(1024)S(1)}, f32[2048]{0:T(1024)}, u32[]{:S(2)}) copy-start(f32[2048]{0:T(1024)} %param.13) | copy-start | bytes 24580
  28.9 18.8 %all-to-all-start = ((f32[32,1,128]{2,1,0:T(1,128)}), f32[32,1,128]{2,1,0:T(1,128)S(1)}, u32[]{:S(2)}, u32[]{:S(2)}) async-start(f32[32,1,128]{2,1,0:T(1,128)} %broadcast_in_dim.11), calls=%async_computation | async-start | bytes 32768 | tf_op jit(solution)/shard_map/all_to_all | solution.py:211
  35.4 0.7 copy-start.14
  36.1 0.7 copy-start.16
  36.8 0.6 copy-start.20
  37.5 0.6 copy-start.22
  38.1 0.6 copy-start.24
  38.7 1.0 %copy-start.13 = (f32[2,64,512]{2,1,0:T(8,128)S(1)}, f32[2,64,512]{2,1,0:T(8,128)}, u32[]{:S(2)}) copy-start(f32[2,64,512]{2,1,0:T(8,128)} %copy-done.12) | copy-start | bytes 786436
  39.7 0.9 %copy-start.15 = (f32[2,64,512]{2,1,0:T(8,128)S(1)}, f32[2,64,512]{2,1,0:T(8,128)}, u32[]{:S(2)}) copy-start(f32[2,64,512]{2,1,0:T(8,128)} %copy-done.14) | copy-start | bytes 786436
  40.6 0.9 %copy-start.17 = (f32[2,64,512]{2,1,0:T(8,128)S(1)}, f32[2,64,512]{2,1,0:T(8,128)}, u32[]{:S(2)}) copy-start(f32[2,64,512]{2,1,0:T(8,128)} %copy-done.16) | copy-start | bytes 786436
  41.6 0.9 %copy-start.19 = (f32[136,128]{1,0:T(8,128)S(1)}, f32[136,128]{1,0:T(8,128)}, u32[]{:S(2)}) copy-start(f32[136,128]{1,0:T(8,128)} %copy-done.18) | copy-start | bytes 208900
  42.5 0.9 %copy-start.21 = (f32[136,128]{1,0:T(8,128)S(1)}, f32[136,128]{1,0:T(8,128)}, u32[]{:S(2)}) copy-start(f32[136,128]{1,0:T(8,128)} %copy-done.20) | copy-start | bytes 208900
  43.3 0.9 %copy-start.23 = (f32[136,128]{1,0:T(8,128)S(1)}, f32[136,128]{1,0:T(8,128)}, u32[]{:S(2)}) copy-start(f32[136,128]{1,0:T(8,128)} %copy-done.22) | copy-start | bytes 208900
  44.2 0.9 %copy-start.25 = (f32[136,128]{1,0:T(8,128)S(1)}, f32[136,128]{1,0:T(8,128)}, u32[]{:S(2)}) copy-start(f32[136,128]{1,0:T(8,128)} %copy-done.24) | copy-start | bytes 208900
  46.7 1.0 %copy-start.8 = (f32[2,512,256]{2,1,0:T(8,128)}, f32[2,512,256]{2,1,0:T(8,128)S(1)}, u32[]{:S(2)}) copy-start(f32[2,512,256]{2,1,0:T(8,128)S(1)} %get-tuple-element.37.grad) | copy-start | bytes 3145732
  47.7 1.2 %copy-start.9 = (f32[2,512,256]{2,1,0:T(8,128)S(1)}, f32[2,512,256]{2,1,0:T(8,128)}, u32[]{:S(2)}) copy-start(f32[2,512,256]{2,1,0:T(8,128)} %copy-done.8) | copy-start | bytes 3145732
  73.0 8.8 %copy-start.7 = (f32[64,2048]{1,0:T(8,128)S(1)}, f32[64,2048]{1,0:T(8,128)}, u32[]{:S(2)}) copy-start(f32[64,2048]{1,0:T(8,128)} %right_plan.3) | copy-start | bytes 1572868
  73.0 8.8 %copy-start.11 = (f32[64,2048]{1,0:T(8,128)S(1)}, f32[64,2048]{1,0:T(8,128)}, u32[]{:S(2)}) copy-start(f32[64,2048]{1,0:T(8,128)} %copy-done.10) | copy-start | bytes 1572868
  73.6 8.2 %copy-start.5 = (f32[64,2048]{1,0:T(8,128)S(1)}, f32[64,2048]{1,0:T(8,128)}, u32[]{:S(2)}) copy-start(f32[64,2048]{1,0:T(8,128)} %left_plan.3) | copy-start | bytes 1572868
  74.2 10.0 %all-to-all-start.3 = ((f32[32,4,128]{2,1,0:T(4,128)}), f32[32,4,128]{2,1,0:T(4,128)S(1)}, u32[]{:S(2)}, u32[]{:S(2)}) async-start(f32[32,4,128]{2,1,0:T(4,128)} %broadcast_in_dim.14), calls=%async_computation.3 | async-start | bytes 131072 | tf_op jit(solution)/shard_map/all_to_all | solution.py:211
  77.0 3.7 %collective-permute-start.10 = (f32[2,512]{1,0:T(2,128)S(1)}, f32[2,512]{1,0:T(2,128)S(1)}, u32[]{:S(2)}, u32[]{:S(2)}) collective-permute-start(f32[2,512]{1,0:T(2,128)S(1)} %shard_map.100.refs_0_), channel_id=1, source_target_pairs={{2,0},{3,1},{0,2},{1,3},{6,4},{7,5},{4,6},{5,7},{10,8},{11,9},{8,1... | collective-permute-start | bytes 12296 | tf_op jit(solution)/shard_map/ppermute | solution.py:214
  78.6 3.0 %collective-permute-start.11 = (f32[2,512]{1,0:T(2,128)S(1)}, f32[2,512]{1,0:T(2,128)S(1)}, u32[]{:S(2)}, u32[]{:S(2)}) collective-permute-start(f32[2,512]{1,0:T(2,128)S(1)} %shard_map.100.refs_0_), channel_id=1, source_target_pairs={{3,0},{0,1},{1,2},{2,3},{7,4},{4,5},{5,6},{6,7},{11,8},{8,9},{9,10... | collective-permute-start | bytes 12296 | tf_op jit(solution)/shard_map/ppermute | solution.py:214
  78.6 3.1 %collective-permute-start.9 = (f32[2,512]{1,0:T(2,128)S(1)}, f32[2,512]{1,0:T(2,128)S(1)}, u32[]{:S(2)}, u32[]{:S(2)}) collective-permute-start(f32[2,512]{1,0:T(2,128)S(1)} %shard_map.100.refs_0_), channel_id=1, source_target_pairs={{1,0},{2,1},{3,2},{0,3},{5,4},{6,5},{7,6},{4,7},{9,8},{10,9},{11,1... | collective-permute-start | bytes 12296 | tf_op jit(solution)/shard_map/ppermute | solution.py:214

commit v3 on v2

v3 whole, which is shorter than its diff:
```python
import functools

import jax
import jax.numpy as jnp
from jax import lax
from jax.experimental import pallas as pl
from jax.experimental.pallas import tpu as pltpu
from jax.sharding import PartitionSpec as P

RANK = 256
ITERS = 3
LANES = 128


def dot(a, b, a_dim, b_dim):
    return lax.dot_general(
        a, b, (((a_dim,), (b_dim,)), ((), ())), preferred_element_type=jnp.float32
    )


HBM = pl.BlockSpec(memory_space=pltpu.HBM)
VMEM = pl.BlockSpec(memory_space=pltpu.VMEM)


def call(body, outs, args, scratch=(), aliases=None):
    specs = [pl.BlockSpec(memory_space=pltpu.SMEM)]
    specs += [spec for _, spec in args[1:]]
    return pl.pallas_call(
        body,
        out_shape=[shape for shape, _ in outs],
        in_specs=specs,
        out_specs=[spec for _, spec in outs],
        scratch_shapes=list(scratch),
        input_output_aliases=aliases or {},
        compiler_params=pltpu.CompilerParams(vmem_limit_bytes=16 * 2**20),
    )(args[0], *[array for array, _ in args[1:]])


def on_chip(*arrays):
    return [(array, VMEM) for array in arrays]


def anywhere(*arrays):
    return [(array, pl.BlockSpec(memory_space=pl.ANY)) for array in arrays]


def in_hbm(*arrays):
    pinned = [
        array if isinstance(array, jax.ShapeDtypeStruct) else pltpu.with_memory_space_constraint(array, pltpu.HBM)
        for array in arrays
    ]
    return [(array, HBM) for array in pinned]


def f32(*shape):
    return jax.ShapeDtypeStruct(shape, jnp.float32)


def project(n_rank, at, left_factor, right_factor, left_plan, right_plan, left_mass, right_mass, log_inner, *refs):
    sums, left_kept, right_kept, log_kept = refs[:4]
    blocks = refs[4 : 4 + n_rank]
    masses, done = refs[4 + n_rank :]
    depth = left_factor.shape[0]
    columns = left_plan.shape[0]
    span = left_plan.shape[1] // n_rank
    starts = [pl.multiple_of(((at[0] + shift) % n_rank) * span, LANES) for shift in range(n_rank)]
    pairs = [(right_factor, right_kept), (left_factor, left_kept)]
    for side, plan in ((1, right_plan), (0, left_plan)):
        for shift in range(n_rank):
            pairs.append((plan.at[:, pl.ds(starts[shift], span)], blocks[shift].at[side]))
    pairs += [
        (left_mass, masses.at[0:1]),
        (right_mass, masses.at[1:2]),
        (log_inner, log_kept),
    ]
    copies = [pltpu.make_async_copy(src, dst, done.at[i]) for i, (src, dst) in enumerate(pairs)]
    for copy in copies:
        copy.start()
    for side, kept in ((1, right_kept), (0, left_kept)):
        copies[1 - side].wait()
        total = jnp.zeros((depth, columns), jnp.float32)
        for shift in range(n_rank):
            copies[2 + (1 - side) * n_rank + shift].wait()
            here = kept[:, pl.ds(starts[shift], span)]
            total = total + dot(here, blocks[shift][side].astype(jnp.bfloat16), 1, 1)
        place = slice(0, columns) if side else slice(columns, 2 * columns)
        sums[:depth, place] = total
    for copy in copies[2 + 2 * n_rank :]:
        copy.wait()
    sums[depth:, :columns] = jnp.full((8, columns), jnp.sum(masses[0:1]))
    sums[depth:, columns:] = jnp.full((8, columns), jnp.sum(masses[1:2]))


def gradients(at, sums, log_inner, left_factor, right_factor, scaled, top):
    depth = left_factor.shape[0]
    columns = log_inner.shape[1]
    total_left = sums[depth : depth + 1, :columns]
    inner = total_left / RANK * jnp.exp(log_inner[...])
    proj_left = sums[:depth, columns:]
    scaled_right = (sums[:depth, :columns] / inner).astype(jnp.bfloat16)
    scaled_left = (proj_left / inner).astype(jnp.bfloat16)
    right = scaled_right.astype(jnp.float32)
    scaled[:depth, :columns] = right
    scaled[:depth, columns:] = scaled_left.astype(jnp.float32)
    pairing = jnp.sum(right * proj_left, axis=0, keepdims=True)
    grad_inner = -pairing / inner
    scaled[depth:, :columns] = jnp.broadcast_to(inner, (8, columns))
    scaled[depth:, columns:] = jnp.broadcast_to(grad_inner, (8, columns))
    peak = jnp.max(jnp.abs(grad_inner))
    peak = jnp.maximum(peak, jnp.max(jnp.abs(dot(scaled_right, left_factor[...], 0, 0))))
    peak = jnp.maximum(peak, jnp.max(jnp.abs(dot(scaled_left, right_factor[...], 0, 0))))
    top[...] = jnp.full(top.shape, peak)


def as_column(row):
    return jnp.broadcast_to(row, (LANES, row.shape[1])).T


def turn(n_rank, at, sums, left_factor, right_factor, left_mass, right_mass, *refs):
    scaled_in = refs[:n_rank]
    plans_in = refs[n_rank : 2 * n_rank]
    plan_out, grad_out, mass_out, inner_out, factors, masses, scaled, plans, done = refs[2 * n_rank :]
    depth = left_factor.shape[0]
    columns = sums.shape[1] // 2
    span = left_factor.shape[1] // n_rank
    here = pl.ds(pl.multiple_of(at[0] * span, LANES), span)
    pairs = [(plans_in[s], plans.at[s]) for s in range(n_rank)]
    pairs += [(left_mass.at[:, here], masses.at[0]), (right_mass.at[:, here], masses.at[1])]
    early = len(pairs)
    pairs += [(left_factor.at[:, here], factors.at[0]), (right_factor.at[:, here], factors.at[1])]
    pairs += [(scaled_in[s], scaled.at[s]) for s in range(n_rank)]
    copies = [pltpu.make_async_copy(src, dst, done.at[i]) for i, (src, dst) in enumerate(pairs)]
    for copy in copies:
        copy.start()
    for copy in copies[:early]:
        copy.wait()
    for side in range(2):
        plan_out[side] = jnp.concatenate([plans[s, side].T for s in range(n_rank)], axis=1)
    ratio = sums[depth : depth + 1, :1] / sums[depth : depth + 1, columns : columns + 1]
    mass_out[0] = as_column(masses[0])
    mass_out[1] = as_column(masses[1] * ratio)
    for copy in copies[early:]:
        copy.wait()
    right = jnp.concatenate([scaled[s, :depth, :columns] for s in range(n_rank)], axis=1)
    left = jnp.concatenate([scaled[s, :depth, columns:] for s in range(n_rank)], axis=1)
    grad_out[0] = dot(factors[0], right.astype(jnp.bfloat16), 0, 0)
    grad_out[1] = dot(factors[1], left.astype(jnp.bfloat16), 0, 0)
    for row, place in ((0, slice(0, columns)), (1, slice(columns, 2 * columns))):
        parts = [scaled[s, depth : depth + 1, place] for s in range(n_rank)]
        inner_out[row : row + 1] = jnp.concatenate(parts, axis=1)


def rolled(pair, shift):
    rows = jnp.concatenate([pair[0], pair[1]] * 4, axis=0)
    return pltpu.roll(rows, shift, 1)


def totals(n_rank, at, side_sum, all_k, columns):
    both = jnp.sum(side_sum[...], axis=0)
    half = all_k // LANES
    left = jnp.concatenate([both[i : i + 1] for i in range(half)], axis=1)
    right = jnp.concatenate([both[half + i : half + i + 1] for i in range(half)], axis=1)
    moved = rolled((left, right), ((n_rank - at[0]) % n_rank) * columns)
    return moved[0:1], moved[1:2]


def sweep(n_rank, at, columns, tilted, mass, scales, part, rows=None):
    got = []
    for side in range(2):
        block = tilted[side]
        weighted = block if scales is None else block * scales[side]
        row = mass[side] / jnp.sum(weighted, axis=1, keepdims=True)
        if rows is not None:
            rows[side] = row
        got.append(jnp.sum(block * row[:, :1], axis=0, keepdims=True))
    moved = rolled(got, at[0] * columns)
    half = moved.shape[1] // LANES
    pieces = [
        moved[side : side + 1, i * LANES : (i + 1) * LANES] for side in range(2) for i in range(half)
    ]
    part[...] = jnp.broadcast_to(jnp.concatenate(pieces, axis=0)[None], part.shape)


def balance(inner, scales, sums):
    mixed = jnp.log(inner) + jnp.log(scales[0] * sums[0]) + jnp.log(scales[1] * sums[1])
    inner = jnp.exp(mixed / 3.0)
    return inner, (inner / sums[0], inner / sums[1])


def step_of(tops):
    return 5.0 / jnp.maximum(jnp.max(tops[...]), 0.25)


def tilt(n_rank, columns, at, tops, plan, grad, mass, inner_in, tilted, inner_out, part):
    step = step_of(tops)
    for side in range(2):
        tilted[side] = plan[side] * jnp.exp(-step * grad[side])
    inner_out[0:1] = inner_in[0:1] * jnp.exp(-step * inner_in[1:2])
    sweep(n_rank, at, columns, tilted, mass, None, part)


def again(n_rank, columns, first, at, parts, tilted, mass, state_in, state_out, part, rows=None):
    all_k = tilted.shape[2]
    sums = totals(n_rank, at, parts, all_k, columns)
    ones = jnp.ones((1, all_k), jnp.float32)
    old = (ones, ones) if first else (state_in[1:2], state_in[2:3])
    inner, scales = balance(state_in[0:1], old, sums)
    state_out[0:1] = inner
    state_out[1:2] = scales[0]
    state_out[2:3] = scales[1]
    sweep(n_rank, at, columns, tilted, mass, scales, part, rows)


def lay_rows(at, rows, flat):
    for side in range(2):
        flat[side : side + 1] = rows[side].T[0:1]


def own_points(n_rank, at, tops, scaled, left_factor, right_factor, left_plan, right_plan, *refs):
    flats = refs[:n_rank]
    left, right, left_in, right_in, left_was, right_was, done = refs[n_rank:]
    pairs = [
        (left_factor, left_in),
        (right_factor, right_in),
        (left_plan, left_was),
        (right_plan, right_was),
    ]
    copies = [pltpu.make_async_copy(src, dst, done.at[i]) for i, (src, dst) in enumerate(pairs)]
    for copy in copies:
        copy.start()
    step = step_of(tops)
    depth = left_factor.shape[0]
    columns, points = left_plan.shape
    span = points // n_rank
    scaled_right = scaled[:depth, :columns].astype(jnp.bfloat16)
    scaled_left = scaled[:depth, columns:].astype(jnp.bfloat16)
    for copy in copies:
        copy.wait()
    for shift in range(n_rank):
        start = pl.multiple_of(((at[0] + shift) % n_rank) * span, LANES)
        here = pl.ds(start, span)
        row = flats[shift]
        up = dot(scaled_right, left_in[:, here], 0, 0)
        left[:, here] = row[0:1] * (left_was[:, here] * jnp.exp(-step * up))
        up = dot(scaled_left, right_in[:, here], 0, 0)
        right[:, here] = row[1:2] * (right_was[:, here] * jnp.exp(-step * up))


def finish(n_rank, columns, at, parts, state, sums, left, right, new_left, new_right, new_log, left_out, right_out, done):
    all_k = state.shape[1]
    got = totals(n_rank, at, parts, all_k, columns)
    inner, scales = balance(state[0:1], (state[1:2], state[2:3]), got)
    depth = sums.shape[0] - 8
    copies = []
    for side, (was, out, new) in enumerate(((left, left_out, new_left), (right, right_out, new_right))):
        out[...] = was[...] * as_column(scales[side])[:columns, :1]
        copies.append(pltpu.make_async_copy(out, new, done.at[side]))
        copies[-1].start()
    new_log[...] = jnp.log(inner[:, :columns]) - jnp.log(sums[depth : depth + 1, :columns] / RANK)
    for copy in copies:
        copy.wait()


def solution(mesh):
    n_rows = mesh.shape["rows"]
    n_rank = mesh.shape["rank"]
    everyone = ("rows", "rank")
    n_all = n_rows * n_rank

    def sum_over_rows(value):
        if n_rows & (n_rows - 1):
            return lax.psum(value, "rows")
        stride = 1
        while stride < n_rows:
            pairs = [(i, i ^ stride) for i in range(n_rows)]
            value = value + lax.ppermute(value, "rows", pairs)
            stride *= 2
        return value

    def to_everyone(value):
        return lax.all_to_all(value, everyone, 0, 0)

    def from_rank(value, shift):
        return lax.ppermute(value, "rank", [((i + shift) % n_rank, i) for i in range(n_rank)])

    def per_device(left_factor, right_factor, left_plan, right_plan, log_inner, left_mass, right_mass):
        depth, points = left_factor.shape
        columns = left_plan.shape[0]
        all_k = columns * n_rank
        span = points // n_rank
        at = lax.axis_index("rank").reshape(1)
        arguments = (
            left_factor, right_factor, left_plan, right_plan,
            left_mass.reshape(1, points), right_mass.reshape(1, points), log_inner.reshape(1, columns),
        )
        factor_shape = jax.ShapeDtypeStruct((depth, points), jnp.bfloat16)
        sums_shape = f32(depth + 8, 2 * columns)
        sums, left_kept, right_kept, log_kept, *blocks = call(
            functools.partial(project, n_rank),
            on_chip(sums_shape, factor_shape, factor_shape, f32(1, columns))
            + on_chip(*[f32(2, columns, span)] * n_rank),
            [at, *in_hbm(*arguments)],
            [pltpu.VMEM((2, points), jnp.float32), pltpu.SemaphoreType.DMA((5 + 2 * n_rank,))],
        )
        plans = [blocks[0]]
        for shift in range(1, n_rank):
            plans.append(
                lax.ppermute(blocks[shift], "rank", [(i, (i + shift) % n_rank) for i in range(n_rank)])
            )
        plans = [plans[(n_rank - s) % n_rank] for s in range(n_rank)]
        sums = sum_over_rows(sums)
        scaled, top = call(
            gradients,
            on_chip(sums_shape, f32(n_all, 1, LANES)),
            [at, *on_chip(sums, log_kept, left_kept, right_kept)],
        )
        tops = to_everyone(top)
        scaleds = [scaled] + [from_rank(scaled, s) for s in range(1, n_rank)]
        plan, grad, mass, inner = call(
            functools.partial(turn, n_rank),
            on_chip(f32(2, span, all_k), f32(2, span, all_k), f32(2, span, LANES), f32(8, all_k)),
            [at, *on_chip(sums), *in_hbm(*arguments[:2], *arguments[4:6]), *anywhere(*scaleds, *plans)],
            [
                pltpu.VMEM((2, depth, span), jnp.bfloat16),
                pltpu.VMEM((2, 1, span), jnp.float32),
                pltpu.VMEM((n_rank, depth + 8, 2 * columns), jnp.float32),
                pltpu.VMEM((n_rank, 2, columns, span), jnp.float32),
                pltpu.SemaphoreType.DMA((4 + 2 * n_rank,)),
            ],
        )
        part_shape = f32(n_all, 2 * all_k // LANES, LANES)
        tilted, state, part = call(
            functools.partial(tilt, n_rank, columns),
            on_chip(f32(2, span, all_k), f32(8, all_k), part_shape),
            [at, *on_chip(tops, plan, grad, mass, inner)],
            aliases={2: 0},
        )
        for repeat in range(1, ITERS):
            last = repeat == ITERS - 1
            parts = to_everyone(part)
            state, part, *rows = call(
                functools.partial(again, n_rank, columns, repeat == 1),
                on_chip(f32(8, all_k), part_shape, *[f32(2, span, LANES)] * last),
                [at, *on_chip(parts, tilted, mass, state)],
            )
        parts = to_everyone(part)
        (flat,) = call(lay_rows, on_chip(f32(2, span)), [at, *on_chip(*rows)])
        flats = [flat] + [from_rank(flat, s) for s in range(1, n_rank)]
        left, right = call(
            functools.partial(own_points, n_rank),
            on_chip(f32(columns, points), f32(columns, points)),
            [at, *on_chip(tops, scaled), *in_hbm(left_factor, right_factor, left_plan, right_plan), *on_chip(*flats)],
            [pltpu.VMEM((depth, points), jnp.bfloat16)] * 2
            + [pltpu.VMEM((columns, points), jnp.float32)] * 2
            + [pltpu.SemaphoreType.DMA((4,))],
        )
        new_left, new_right, new_log = call(
            functools.partial(finish, n_rank, columns),
            [*in_hbm(f32(columns, points), f32(columns, points)), *on_chip(f32(1, columns))],
            [at, *on_chip(parts, state, sums, left, right)],
            [pltpu.VMEM((columns, points), jnp.float32)] * 2 + [pltpu.SemaphoreType.DMA((2,))],
        )
        return (new_left, new_right, new_log.reshape(columns))

    in_specs = (
        P(None, "rows"),
        P(None, "rows"),
        P("rank", "rows"),
        P("rank", "rows"),
        P("rank"),
        P("rows"),
        P("rows"),
    )
    out_specs = (P("rank", "rows"), P("rank", "rows"), P("rank"))
    return jax.shard_map(
        per_device, mesh=mesh, in_specs=in_specs, out_specs=out_specs, check_vma=False
    )
```

time: 86.4 us -> 76.6 us (0.89)
  local copies, waits for them, and re-layouts: 21.5 us -> 6.2 us
  Pallas kernels: 7.68 us -> 14.5 us
  waiting for transfers between devices: 11 us -> 8.9 us
  starting transfers between devices: 22.4 us -> 23.4 us
    unnamed x60 -> x16, local copies, waits for them, and re-layouts: 20.2 us -> 6.2 us
    pallas_call x9, Pallas kernels: 7.68 us -> 14.5 us  [call(): pl.pallas_call(body, out_shape=[shape for shape, _ in outs], in_specs=spe...]
    all_to_all x2, waiting for transfers between devices: 2.11 us -> 0.08 us  [to_everyone(): return lax.all_to_all(value, everyone, 0, 0)]
    broadcast_in_dim x4 -> x0, local copies, waits for them, and re-layouts: 1.27 us -> none  [to_everyone(): spread = jnp.broadcast_to(value[None], (n_all,) + value.shape)]
    ppermute x6, starting transfers between devices: 4.51 us -> 5.45 us  [from_rank(): lax.ppermute(value, 'rank', [((i + shift) % n_rank, i) for i in range(n_r...]
  transfers between devices with their start and end apart: 14 -> 14, of which waited for: 6 -> 6; matrix products, arithmetic and copies ran while one was open for 1% -> 0% of each run, Pallas kernels for 3% -> 8%
where the time goes in v3:
time: 76.6 us; the launch traced here: 75.8 us
  starting transfers between devices  23.4 us (31%)
  blocking collectives  22.1 us (29%)
  Pallas kernels  14.5 us (19%)
  waiting for transfers between devices  8.9 us (12%)
  local copies, waits for them, and re-layouts  6.2 us (8%)
    all_to_all x2, blocking collectives, to_everyone(): return lax.all_to_all(value, everyone, 0, 0)  22.1 us
    pallas_call x9, Pallas kernels, call(): pl.pallas_call(body, out_shape=[shape for shape, _ in outs], in_specs=spe...  14.5 us
    all_to_all x2, starting transfers between devices, to_everyone(): return lax.all_to_all(value, everyone, 0, 0)  8.98 us
    ppermute x3, waiting for transfers between devices, sum_over_rows(): value = value + lax.ppermute(value, 'rows', pairs)  7.48 us
    unnamed x16, local copies, waits for them, and re-layouts  6.2 us
    ppermute x3, starting transfers between devices, sum_over_rows(): value = value + lax.ppermute(value, 'rows', pairs)  5.82 us
    ppermute x6, starting transfers between devices, from_rank(): lax.ppermute(value, 'rank', [((i + shift) % n_rank, i) for i in range(n_r...  5.45 us
    ppermute x3, starting transfers between devices, per_device(): lax.ppermute(blocks[shift], 'rank', [(i, (i + shift) % n_rank) for i in r...  3.1 us
  transfers between devices with their start and end apart: 14, of which 6 were waited for; matrix products, arithmetic and copies ran while one was open for 0% of the time, Pallas kernels for 8%

profile of v3, /device:TPU:0, one launch (start us, length us, event | category | flops | bytes accessed | tf_op | source)
XLA Modules:
  0.0 75.8 jit_solution(8826273147678778014)
XLA Ops:
  0.6 2.5 %shard_map.94 = (f32[136,128]{1,0:T(8,128)S(1)}, bf16[128,2048]{1,0:T(8,128)(2,1)S(1)}, bf16[128,2048]{1,0:T(8,128)(2,1)S(1)}, f32[1,64]{1,0:T(1,128)S(1)}, f32[...) custom-call(s32[1]{0:T(128)} %bitcast.at, ...), custom_call_target="tpu_custom_call" | custom-call | tf_op jit(solution)/shard_map/pallas_call | solution.py:28
  3.1 2.5 %collective-permute-start.6 = (f32[2,64,512]{2,1,0:T(8,128)S(1)}, f32[2,64,512]{2,1,0:T(8,128)S(1)}, u32[]{:S(2)}, u32[]{:S(2)}) collective-permute-start(f32[2,64,512]{2,1,0:T(8,128)S(1)} %get-tuple-element.37), channel_id=1, source_target_pairs={{0,3},{1,0},{2,1},{3,2},{4,7},{5,4},{6,5},{7,6},{8,11},{9,8},{10,9... | collective-permute-start | bytes 786440 | tf_op jit(solution)/shard_map/ppermute | solution.py:308
  5.6 1.5 %collective-permute-start = (f32[136,128]{1,0:T(8,128)S(1)}, f32[136,128]{1,0:T(8,128)S(1)}, u32[]{:S(2)}, u32[]{:S(2)}) collective-permute-start(f32[136,128]{1,0:T(8,128)S(1)} %get-tuple-element.30), channel_id=1, source_target_pairs={{0,4},{4,0},{8,12},{12,8},{16,20},{20,16},{24,28},{28,24},{1,5},{5... | collective-permute-start | bytes 208904 | tf_op jit(solution)/shard_map/ppermute | solution.py:276
  7.1 0.6 collective-permute-start.7
  7.8 0.0 collective-permute-start.8
  7.8 2.1 %collective-permute-done = f32[136,128]{1,0:T(8,128)S(1)} collective-permute-done((f32[136,128]{1,0:T(8,128)S(1)}, f32[136,128]{1,0:T(8,128)S(1)}, u32[]{:S(2)}, u32[]{:S(2)}) %collective-permute-start) | collective-permute-done | bytes 69664 | tf_op jit(solution)/shard_map/ppermute | solution.py:276
  9.9 1.6 %collective-permute-start.1 = (f32[136,128]{1,0:T(8,128)S(1)}, f32[136,128]{1,0:T(8,128)S(1)}, u32[]{:S(2)}, u32[]{:S(2)}) collective-permute-start(f32[136,128]{1,0:T(8,128)S(1)} %add.9), channel_id=1, source_target_pairs={{0,8},{4,12},{8,0},{12,4},{16,24},{20,28},{24,16},{28,20},{1,9},{5... | collective-permute-start | bytes 208904 | tf_op jit(solution)/shard_map/ppermute | solution.py:276
  11.6 2.7 %collective-permute-done.1 = f32[136,128]{1,0:T(8,128)S(1)} collective-permute-done((f32[136,128]{1,0:T(8,128)S(1)}, f32[136,128]{1,0:T(8,128)S(1)}, u32[]{:S(2)}, u32[]{:S(2)}) %collective-permute-start.1) | collective-permute-done | bytes 69664 | tf_op jit(solution)/shard_map/ppermute | solution.py:276
  14.3 2.7 %collective-permute-start.2 = (f32[136,128]{1,0:T(8,128)S(1)}, f32[136,128]{1,0:T(8,128)S(1)}, u32[]{:S(2)}, u32[]{:S(2)}) collective-permute-start(f32[136,128]{1,0:T(8,128)S(1)} %add.10), channel_id=1, source_target_pairs={{0,16},{4,20},{8,24},{12,28},{16,0},{20,4},{24,8},{28,12},{1,17},{... | collective-permute-start | bytes 208904 | tf_op jit(solution)/shard_map/ppermute | solution.py:276
  17.0 2.6 %collective-permute-done.2 = f32[136,128]{1,0:T(8,128)S(1)} collective-permute-done((f32[136,128]{1,0:T(8,128)S(1)}, f32[136,128]{1,0:T(8,128)S(1)}, u32[]{:S(2)}, u32[]{:S(2)}) %collective-permute-start.2) | collective-permute-done | bytes 69664 | tf_op jit(solution)/shard_map/ppermute | solution.py:276
  19.6 1.2 %shard_map.95 = (f32[136,128]{1,0:T(8,128)S(1)}, f32[32,1,128]{2,1,0:T(1,128)}) custom-call(s32[1]{0:T(128)} %bitcast.at, f32[136,128]{1,0:T(8,128)S(1)} %add.11.sums, f32[1,64]{1,0:T(1,128)S(1)} %get-tuple-element.31.log_inner, bf16[128,2048]{1,0:T(8,128)(2,1)S(1)} %get-tuple-element.32.left_factor, bf16[128,2048]{1,0:T(8,128)(2,1)S(1)} %get-tuple-element.33.right_factor), custom_call_target="tpu_custom_call" | custom-call | tf_op jit(solution)/shard_map/pallas_call | solution.py:28
  20.8 0.0 collective-permute-start.5
  20.8 0.9 %collective-permute-start.4 = (f32[136,128]{1,0:T(8,128)S(1)}, f32[136,128]{1,0:T(8,128)S(1)}, u32[]{:S(2)}, u32[]{:S(2)}) collective-permute-start(f32[136,128]{1,0:T(8,128)S(1)} %get-tuple-element.35.refs_0_.scaled), channel_id=1, source_target_pairs={{2,0},{3,1},{0,2},{1,3},{6,4},{7,5},{4,6},{5,7},{10,8},{11,9},{8,1... | collective-permute-start | bytes 208904 | tf_op jit(solution)/shard_map/ppermute | solution.py:284
  21.6 0.0 collective-permute-done.6.refs_5_
  21.6 1.5 %collective-permute-start.3 = (f32[136,128]{1,0:T(8,128)S(1)}, f32[136,128]{1,0:T(8,128)S(1)}, u32[]{:S(2)}, u32[]{:S(2)}) collective-permute-start(f32[136,128]{1,0:T(8,128)S(1)} %get-tuple-element.35.refs_0_.scaled), channel_id=1, source_target_pairs={{1,0},{2,1},{3,2},{0,3},{5,4},{6,5},{7,6},{4,7},{9,8},{10,9},{11,1... | collective-permute-start | bytes 208904 | tf_op jit(solution)/shard_map/ppermute | solution.py:284
  23.1 6.4 %all-to-all-start = ((f32[32,1,128]{2,1,0:T(1,128)}), f32[32,1,128]{2,1,0:T(1,128)}, u32[]{:S(2)}, u32[]{:S(2)}) async-start(f32[32,1,128]{2,1,0:T(1,128)} %get-tuple-element.34), calls=%async_computation | async-start | bytes 32768 | tf_op jit(solution)/shard_map/all_to_all | solution.py:281
  29.5 0.0 collective-permute-done.7.refs_6_
  29.5 0.0 collective-permute-done.8.refs_7_
  29.5 0.0 copy-start
  29.5 0.7 copy-done
  30.2 0.0 collective-permute-done.5.refs_3_
  30.2 0.6 copy-done.2
  30.9 0.0 collective-permute-done.4.refs_2_
  30.9 0.6 copy-done.4
  31.5 0.0 collective-permute-done.3.refs_1_
  31.5 0.6 copy-done.6
  32.2 0.9 %copy-done.1 = f32[2,64,512]{2,1,0:T(8,128)S(1)} copy-done((f32[2,64,512]{2,1,0:T(8,128)S(1)}, f32[2,64,512]{2,1,0:T(8,128)}, u32[]{:S(2)}) %copy-start.1) | copy-done | bytes 262168
  33.1 0.9 %copy-done.3 = f32[136,128]{1,0:T(8,128)S(1)} copy-done((f32[136,128]{1,0:T(8,128)S(1)}, f32[136,128]{1,0:T(8,128)}, u32[]{:S(2)}) %copy-start.3) | copy-done | bytes 69656
  34.0 0.9 %copy-done.5 = f32[136,128]{1,0:T(8,128)S(1)} copy-done((f32[136,128]{1,0:T(8,128)S(1)}, f32[136,128]{1,0:T(8,128)}, u32[]{:S(2)}) %copy-start.5) | copy-done | bytes 69656
  34.9 0.9 %copy-done.7 = f32[136,128]{1,0:T(8,128)S(1)} copy-done((f32[136,128]{1,0:T(8,128)S(1)}, f32[136,128]{1,0:T(8,128)}, u32[]{:S(2)}) %copy-start.7) | copy-done | bytes 69656
  35.8 2.4 %shard_map.96 = (f32[2,512,256]{2,1,0:T(8,128)S(1)}, f32[2,512,256]{2,1,0:T(8,128)S(1)}, f32[2,512,128]{2,1,0:T(8,128)S(1)}, f32[8,256]{1,0:T(8,128)S(1)}) custom-call(s32[1]{0:T(128)} %bitcast.at, f32[136,128]{1,0:T(8,128)S(1)} %add.11.sums, bf16[128,2048]{1,0:T(8,128)(2,1)} %left_factor.5, bf16[128,2048]{1,0:T(8,128)(2,1)} %right_factor.5, ...), custom_call_target="tpu_custom_call" | custom-call | tf_op jit(solution)/shard_map/pallas_call | solution.py:28
  38.1 0.0 all-to-all-done.tops
  38.1 1.9 %shard_map.97 = (f32[2,512,256]{2,1,0:T(8,128)S(1)}, f32[8,256]{1,0:T(8,128)S(1)}, f32[32,4,128]{2,1,0:T(4,128)S(1)}) custom-call(s32[1]{0:T(128)} %bitcast.at, f32[32,1,128]{2,1,0:T(1,128)} %all-to-all-done.tops, f32[2,512,256]{2,1,0:T(8,128)S(1)} %get-tuple-element.40.plan, ...), custom_call_target="tpu_custom_call", output_to_operand_aliasing={{0}: (2, {})} | custom-call | tf_op jit(solution)/shard_map/pallas_call | solution.py:28
  40.0 13.0 %all_to_all.20.parts = f32[32,4,128]{2,1,0:T(4,128)S(1)} all-to-all(f32[32,4,128]{2,1,0:T(4,128)S(1)} %get-tuple-element.44), channel_id=1, replica_groups=mesh['rows'=8,'rank'=4] {'rows','rank'}, dimensions={0} | all-to-all | bytes 131072 | tf_op jit(solution)/shard_map/all_to_all | solution.py:281
  53.0 0.6 shard_map.98
  53.6 9.1 %all_to_all.21.parts = f32[32,4,128]{2,1,0:T(4,128)S(1)} all-to-all(f32[32,4,128]{2,1,0:T(4,128)S(1)} %get-tuple-element.47), channel_id=1, replica_groups=mesh['rows'=8,'rank'=4] {'rows','rank'}, dimensions={0} | all-to-all | bytes 131072 | tf_op jit(solution)/shard_map/all_to_all | solution.py:281
  62.7 1.2 %shard_map.99 = (f32[8,256]{1,0:T(8,128)S(1)}, f32[32,4,128]{2,1,0:T(4,128)}, f32[2,512,128]{2,1,0:T(8,128)S(1)}) custom-call(s32[1]{0:T(128)} %bitcast.at, f32[32,4,128]{2,1,0:T(4,128)S(1)} %all_to_all.21.parts, f32[2,512,256]{2,1,0:T(8,128)S(1)} %get-tuple-element.45.tilted, f32[2,512,128]{2,1,0:T(8,128)S(1)} %get-tuple-element.42.mass, ...), custom_call_target="tpu_custom_call" | custom-call | tf_op jit(solution)/shard_map/pallas_call | solution.py:28
  64.0 2.6 %all-to-all-start.3 = ((f32[32,4,128]{2,1,0:T(4,128)}), f32[32,4,128]{2,1,0:T(4,128)S(1)}, u32[]{:S(2)}, u32[]{:S(2)}) async-start(f32[32,4,128]{2,1,0:T(4,128)} %get-tuple-element.49), calls=%async_computation.3 | async-start | bytes 131072 | tf_op jit(solution)/shard_map/all_to_all | solution.py:281
  66.6 0.2 shard_map.100.refs_0_
  66.7 0.1 collective-permute-start.11
  66.9 1.6 %collective-permute-start.10 = (f32[2,512]{1,0:T(2,128)S(1)}, f32[2,512]{1,0:T(2,128)S(1)}, u32[]{:S(2)}, u32[]{:S(2)}) collective-permute-start(f32[2,512]{1,0:T(2,128)S(1)} %shard_map.100.refs_0_), channel_id=1, source_target_pairs={{2,0},{3,1},{0,2},{1,3},{6,4},{7,5},{4,6},{5,7},{10,8},{11,9},{8,1... | collective-permute-start | bytes 12296 | tf_op jit(solution)/shard_map/ppermute | solution.py:284
  68.5 1.3 %collective-permute-start.9 = (f32[2,512]{1,0:T(2,128)S(1)}, f32[2,512]{1,0:T(2,128)S(1)}, u32[]{:S(2)}, u32[]{:S(2)}) collective-permute-start(f32[2,512]{1,0:T(2,128)S(1)} %shard_map.100.refs_0_), channel_id=1, source_target_pairs={{1,0},{2,1},{3,2},{0,3},{5,4},{6,5},{7,6},{4,7},{9,8},{10,9},{11,1... | collective-permute-start | bytes 12296 | tf_op jit(solution)/shard_map/ppermute | solution.py:284
  69.9 0.0 collective-permute-done.11.refs_3_
  69.9 0.6 collective-permute-done.10.refs_2_
  70.5 0.7 collective-permute-done.9.refs_1_
  71.2 2.7 %shard_map.101 = (f32[64,2048]{1,0:T(8,128)S(1)}, f32[64,2048]{1,0:T(8,128)S(1)}) custom-call(s32[1]{0:T(128)} %bitcast.at, f32[32,1,128]{2,1,0:T(1,128)} %all-to-all-done.tops, f32[136,128]{1,0:T(8,128)S(1)} %get-tuple-element.35.refs_0_.scaled, bf16[128,2048]{1,0:T(8,128)(2,1)} %left_factor.5, bf16[128,2048]{1,0:T(8,128)(2,1)} %right_factor.5, ...), custom_call_target="tpu_custom_call" | custom-call | tf_op jit(solution)/shard_map/pallas_call | solution.py:28
  73.9 0.1 all-to-all-done.3.parts
  74.0 1.8 %shard_map.102 = (f32[64,2048]{1,0:T(8,128)}, f32[64,2048]{1,0:T(8,128)}, f32[1,64]{1,0:T(1,128)}) custom-call(s32[1]{0:T(128)} %bitcast.at, f32[32,4,128]{2,1,0:T(4,128)S(1)} %all-to-all-done.3.parts, f32[8,256]{1,0:T(8,128)S(1)} %get-tuple-element.50.state, f32[136,128]{1,0:T(8,128)S(1)} %add.11.sums, f32[64,2048]{1,0:T(8,128)S(1)} %get-tuple-element.52.left, ...), custom_call_target="tpu_custom_call" | custom-call | tf_op jit(solution)/shard_map/pallas_call | solution.py:28
  (10 shorter events, 0.0 us)
Async XLA Ops:
  3.1 18.5 %collective-permute-start.6 = (f32[2,64,512]{2,1,0:T(8,128)S(1)}, f32[2,64,512]{2,1,0:T(8,128)S(1)}, u32[]{:S(2)}, u32[]{:S(2)}) collective-permute-start(f32[2,64,512]{2,1,0:T(8,128)S(1)} %get-tuple-element.37), channel_id=1, source_target_pairs={{0,3},{1,0},{2,1},{3,2},{4,7},{5,4},{6,5},{7,6},{8,11},{9,8},{10,9... | collective-permute-start | bytes 786440 | tf_op jit(solution)/shard_map/ppermute | solution.py:308
  5.6 4.3 %collective-permute-start = (f32[136,128]{1,0:T(8,128)S(1)}, f32[136,128]{1,0:T(8,128)S(1)}, u32[]{:S(2)}, u32[]{:S(2)}) collective-permute-start(f32[136,128]{1,0:T(8,128)S(1)} %get-tuple-element.30), channel_id=1, source_target_pairs={{0,4},{4,0},{8,12},{12,8},{16,20},{20,16},{24,28},{28,24},{1,5},{5... | collective-permute-start | bytes 208904 | tf_op jit(solution)/shard_map/ppermute | solution.py:276
  7.1 22.4 %collective-permute-start.7 = (f32[2,64,512]{2,1,0:T(8,128)S(1)}, f32[2,64,512]{2,1,0:T(8,128)S(1)}, u32[]{:S(2)}, u32[]{:S(2)}) collective-permute-start(f32[2,64,512]{2,1,0:T(8,128)S(1)} %get-tuple-element.38), channel_id=1, source_target_pairs={{0,2},{1,3},{2,0},{3,1},{4,6},{5,7},{6,4},{7,5},{8,10},{9,11},{10,... | collective-permute-start | bytes 786440 | tf_op jit(solution)/shard_map/ppermute | solution.py:308
  7.8 21.8 %collective-permute-start.8 = (f32[2,64,512]{2,1,0:T(8,128)S(1)}, f32[2,64,512]{2,1,0:T(8,128)S(1)}, u32[]{:S(2)}, u32[]{:S(2)}) collective-permute-start(f32[2,64,512]{2,1,0:T(8,128)S(1)} %get-tuple-element.39), channel_id=1, source_target_pairs={{0,1},{1,2},{2,3},{3,0},{4,5},{5,6},{6,7},{7,4},{8,9},{9,10},{10,1... | collective-permute-start | bytes 786440 | tf_op jit(solution)/shard_map/ppermute | solution.py:308
  9.9 4.4 %collective-permute-start.1 = (f32[136,128]{1,0:T(8,128)S(1)}, f32[136,128]{1,0:T(8,128)S(1)}, u32[]{:S(2)}, u32[]{:S(2)}) collective-permute-start(f32[136,128]{1,0:T(8,128)S(1)} %add.9), channel_id=1, source_target_pairs={{0,8},{4,12},{8,0},{12,4},{16,24},{20,28},{24,16},{28,20},{1,9},{5... | collective-permute-start | bytes 208904 | tf_op jit(solution)/shard_map/ppermute | solution.py:276
  14.3 5.3 %collective-permute-start.2 = (f32[136,128]{1,0:T(8,128)S(1)}, f32[136,128]{1,0:T(8,128)S(1)}, u32[]{:S(2)}, u32[]{:S(2)}) collective-permute-start(f32[136,128]{1,0:T(8,128)S(1)} %add.10), channel_id=1, source_target_pairs={{0,16},{4,20},{8,24},{12,28},{16,0},{20,4},{24,8},{28,12},{1,17},{... | collective-permute-start | bytes 208904 | tf_op jit(solution)/shard_map/ppermute | solution.py:276
  20.8 9.5 %collective-permute-start.5 = (f32[136,128]{1,0:T(8,128)S(1)}, f32[136,128]{1,0:T(8,128)S(1)}, u32[]{:S(2)}, u32[]{:S(2)}) collective-permute-start(f32[136,128]{1,0:T(8,128)S(1)} %get-tuple-element.35.refs_0_.scaled), channel_id=1, source_target_pairs={{3,0},{0,1},{1,2},{2,3},{7,4},{4,5},{5,6},{6,7},{11,8},{8,9},{9,10... | collective-permute-start | bytes 208904 | tf_op jit(solution)/shard_map/ppermute | solution.py:284
  20.8 10.1 %collective-permute-start.4 = (f32[136,128]{1,0:T(8,128)S(1)}, f32[136,128]{1,0:T(8,128)S(1)}, u32[]{:S(2)}, u32[]{:S(2)}) collective-permute-start(f32[136,128]{1,0:T(8,128)S(1)} %get-tuple-element.35.refs_0_.scaled), channel_id=1, source_target_pairs={{2,0},{3,1},{0,2},{1,3},{6,4},{7,5},{4,6},{5,7},{10,8},{11,9},{8,1... | collective-permute-start | bytes 208904 | tf_op jit(solution)/shard_map/ppermute | solution.py:284
  21.6 9.9 %collective-permute-start.3 = (f32[136,128]{1,0:T(8,128)S(1)}, f32[136,128]{1,0:T(8,128)S(1)}, u32[]{:S(2)}, u32[]{:S(2)}) collective-permute-start(f32[136,128]{1,0:T(8,128)S(1)} %get-tuple-element.35.refs_0_.scaled), channel_id=1, source_target_pairs={{1,0},{2,1},{3,2},{0,3},{5,4},{6,5},{7,6},{4,7},{9,8},{10,9},{11,1... | collective-permute-start | bytes 208904 | tf_op jit(solution)/shard_map/ppermute | solution.py:284
  23.1 15.0 %all-to-all-start = ((f32[32,1,128]{2,1,0:T(1,128)}), f32[32,1,128]{2,1,0:T(1,128)}, u32[]{:S(2)}, u32[]{:S(2)}) async-start(f32[32,1,128]{2,1,0:T(1,128)} %get-tuple-element.34), calls=%async_computation | async-start | bytes 32768 | tf_op jit(solution)/shard_map/all_to_all | solution.py:281
  29.5 0.7 copy-start
  30.2 0.6 copy-start.2
  30.9 0.6 copy-start.4
  31.5 0.6 copy-start.6
  32.2 0.9 %copy-start.1 = (f32[2,64,512]{2,1,0:T(8,128)S(1)}, f32[2,64,512]{2,1,0:T(8,128)}, u32[]{:S(2)}) copy-start(f32[2,64,512]{2,1,0:T(8,128)} %copy-done) | copy-start | bytes 786436
  33.1 0.9 %copy-start.3 = (f32[136,128]{1,0:T(8,128)S(1)}, f32[136,128]{1,0:T(8,128)}, u32[]{:S(2)}) copy-start(f32[136,128]{1,0:T(8,128)} %copy-done.2) | copy-start | bytes 208900
  34.0 0.9 %copy-start.5 = (f32[136,128]{1,0:T(8,128)S(1)}, f32[136,128]{1,0:T(8,128)}, u32[]{:S(2)}) copy-start(f32[136,128]{1,0:T(8,128)} %copy-done.4) | copy-start | bytes 208900
  34.9 0.9 %copy-start.7 = (f32[136,128]{1,0:T(8,128)S(1)}, f32[136,128]{1,0:T(8,128)}, u32[]{:S(2)}) copy-start(f32[136,128]{1,0:T(8,128)} %copy-done.6) | copy-start | bytes 208900
  64.0 10.0 %all-to-all-start.3 = ((f32[32,4,128]{2,1,0:T(4,128)}), f32[32,4,128]{2,1,0:T(4,128)S(1)}, u32[]{:S(2)}, u32[]{:S(2)}) async-start(f32[32,4,128]{2,1,0:T(4,128)} %get-tuple-element.49), calls=%async_computation.3 | async-start | bytes 131072 | tf_op jit(solution)/shard_map/all_to_all | solution.py:281
  66.7 3.1 %collective-permute-start.11 = (f32[2,512]{1,0:T(2,128)S(1)}, f32[2,512]{1,0:T(2,128)S(1)}, u32[]{:S(2)}, u32[]{:S(2)}) collective-permute-start(f32[2,512]{1,0:T(2,128)S(1)} %shard_map.100.refs_0_), channel_id=1, source_target_pairs={{3,0},{0,1},{1,2},{2,3},{7,4},{4,5},{5,6},{6,7},{11,8},{8,9},{9,10... | collective-permute-start | bytes 12296 | tf_op jit(solution)/shard_map/ppermute | solution.py:284
  66.9 3.6 %collective-permute-start.10 = (f32[2,512]{1,0:T(2,128)S(1)}, f32[2,512]{1,0:T(2,128)S(1)}, u32[]{:S(2)}, u32[]{:S(2)}) collective-permute-start(f32[2,512]{1,0:T(2,128)S(1)} %shard_map.100.refs_0_), channel_id=1, source_target_pairs={{2,0},{3,1},{0,2},{1,3},{6,4},{7,5},{4,6},{5,7},{10,8},{11,9},{8,1... | collective-permute-start | bytes 12296 | tf_op jit(solution)/shard_map/ppermute | solution.py:284
  68.5 2.7 %collective-permute-start.9 = (f32[2,512]{1,0:T(2,128)S(1)}, f32[2,512]{1,0:T(2,128)S(1)}, u32[]{:S(2)}, u32[]{:S(2)}) collective-permute-start(f32[2,512]{1,0:T(2,128)S(1)} %shard_map.100.refs_0_), channel_id=1, source_target_pairs={{1,0},{2,1},{3,2},{0,3},{5,4},{6,5},{7,6},{4,7},{9,8},{10,9},{11,1... | collective-permute-start | bytes 12296 | tf_op jit(solution)/shard_map/ppermute | solution.py:284
